TPU v7x, 1024 devices: a whole 4x4x32 slice. The times are simulated.
1024 devices in a mesh: gx: 32 (over z), gy: 4 (over y), gz: 8 (over x, core).
Axes of the slice: x: 4, y: 4, z: 32, core: 2. Of those that a mesh axis runs over, the one named last changes fastest.
Arguments:
- positions: float32 [3, 128, 16, 1024], P(None, 'gx', 'gy', 'gz'), may hold values from 0.6 to 13.9, as said below
- counts: int32 [128, 16, 16], P('gx', 'gy', 'gz'), may hold values from 24 to 64
Outputs:
- forces: float32 [3, 128, 16, 1024], P(None, 'gx', 'gy', 'gz')
- energy: float32 [128, 16, 1024], P('gx', 'gy', 'gz')
Inputs may be any that keep to these rules, and one draw needn't show every extreme that they name: `positions`: each cell is a box of 2a x 2a x 4a with a = 3.615 and every atom lies inside its own cell's box; two atoms are 1.0 or more apart, and no atom is within 5.51 of an atom outside its cell's 27 neighbour cells.
All inputs are finite; a program needn't handle non-finite values.
Results may differ from a plain program's by a relative error of at most 0.0003.
Values sent between devices are 32-bit elements; how exact they have to be, the bound alone decides.
No kernel may reach another device: no remote copies, remote signals or barrier semaphores. Data moves between devices by JAX's collectives and lax.ppermute only.
A program may use at most 32 MiB of HBM per device.

v0:
```python
import jax
import jax.numpy as jnp
from jax import lax
from jax.sharding import PartitionSpec as P

SLOTS = 64


lattice_const = 3.615
cell_span = (2.0 * lattice_const, 2.0 * lattice_const, 4.0 * lattice_const)
cut_radius = 5.50679
cut_width = 0.50037
dens_scale = 3.80362
beta_one = 0.17394
radius_three = -2.19885
energy_one = 201.458
energy_two = 0.00659288
radius_one = 0.83591
radius_two = 4.46867
alpha_one = 2.97758
alpha_two = 1.54927
shift_delta = 0.0086225
repulsion = ((4.0, 2.24), (40.0, 1.8), (1150.0, 1.2))
embed_zero = -2.28235
embed_curve = 1.35535
lower_terms = (-1.27775, -0.86074, 1.78804, 2.97571)
upper_quartic = 0.4
upper_damping = 0.3
cell_offsets = [
    (first, second, third) for first in (-1, 0, 1) for second in (-1, 0, 1) for third in (-1, 0, 1)
]


def with_halo(value, sides, width):
    for axis, dim in sides:
        count, length = (lax.axis_size(axis), value.shape[dim])
        up = [(i, (i + 1) % count) for i in range(count)]
        down = [(j, i) for i, j in up]
        last = lax.slice_in_dim(value, length - width, length, axis=dim)
        first = lax.slice_in_dim(value, 0, width, axis=dim)
        before = lax.ppermute(last, axis, up)
        after = lax.ppermute(first, axis, down)
        value = jnp.concatenate([before, value, after], axis=dim)
    return value


def tapering(radius):
    scaled = (radius - cut_radius) / cut_width
    quartic = scaled**4
    inside = scaled < 0.0
    taper_value = jnp.where(inside, quartic / (1.0 + quartic), 0.0)
    taper_slope = jnp.where(inside, 4.0 * scaled**3 / (1.0 + quartic) ** 2 / cut_width, 0.0)
    return (taper_value, taper_slope)


def gaussian_part(radius):
    return dens_scale * jnp.exp(-beta_one * (radius - radius_three) ** 2)


def radial_density(radius):
    taper_value, taper_slope = tapering(radius)
    return gaussian_part(radius) * taper_value


def morse_terms(radius, center_at, stiffness):
    decay = jnp.exp(-stiffness * (radius - center_at))
    return (decay * decay - 2.0 * decay, 2.0 * stiffness * (decay - decay * decay))


def pair_terms(radius):
    taper_value, taper_slope = tapering(radius)
    gaussian = gaussian_part(radius)
    dens_value = gaussian * taper_value
    dens_slope = (
        gaussian * (-2.0 * beta_one * (radius - radius_three)) * taper_value
        + gaussian * taper_slope
    )
    morse_first, slope_first = morse_terms(radius, radius_one, alpha_one)
    morse_second, slope_second = morse_terms(radius, radius_two, alpha_two)
    base_value = energy_one * morse_first + energy_two * morse_second + shift_delta
    base_slope = energy_one * slope_first + energy_two * slope_second
    pair_value = base_value * taper_value
    pair_slope = base_slope * taper_value + base_value * taper_slope
    for strength, reach_at in repulsion:
        closeness = jnp.maximum(reach_at - radius, 0.0)
        pair_value = pair_value - strength * closeness**4
        pair_slope = pair_slope + 4.0 * strength * closeness**3
    return (pair_value, pair_slope, dens_value, dens_slope)


def embedding(density):
    excess = density - 1.0
    below_value = (
        embed_zero
        + 0.5 * embed_curve * excess**2
        + lower_terms[0] * excess**3
        + lower_terms[1] * excess**4
        + lower_terms[2] * excess**5
        + lower_terms[3] * excess**6
    )
    below_slope = (
        embed_curve * excess
        + 3.0 * lower_terms[0] * excess**2
        + 4.0 * lower_terms[1] * excess**3
        + 5.0 * lower_terms[2] * excess**4
        + 6.0 * lower_terms[3] * excess**5
    )
    numerator = (
        embed_zero
        + 0.5 * embed_curve * excess**2
        + lower_terms[0] * excess**3
        + upper_quartic * excess**4
    )
    numer_slope = (
        embed_curve * excess + 3.0 * lower_terms[0] * excess**2 + 4.0 * upper_quartic * excess**3
    )
    denominator = 1.0 + upper_damping * excess**3
    above_value = numerator / denominator
    above_slope = (
        numer_slope * denominator - numerator * 3.0 * upper_damping * excess**2
    ) / denominator**2
    is_below = excess < 0.0
    return (
        jnp.where(is_below, below_value, above_value),
        jnp.where(is_below, below_slope, above_slope),
    )


def pair_geometry(center, beside, offset):
    displace = []
    for component in range(3):
        displace.append(
            beside[component][..., None, :]
            + offset[component] * cell_span[component]
            - center[component][..., :, None]
        )
    weight = center[3][..., :, None] * beside[3][..., None, :]
    if offset == (0, 0, 0):
        slot_count = center.shape[-1]
        weight = weight * (1.0 - jnp.eye(slot_count, dtype=jnp.float32))
    squared = displace[0] ** 2 + displace[1] ** 2 + displace[2] ** 2
    radius = jnp.sqrt(jnp.where(weight > 0.0, squared, 100.0))
    return (displace, weight, radius)


def shifted_cells(view_data, offset, extent):
    return view_data[
        :,
        1 + offset[0] : 1 + offset[0] + extent[0],
        1 + offset[1] : 1 + offset[1] + extent[1],
        1 + offset[2] : 1 + offset[2] + extent[2],
    ]


def cell_view(field_data):
    return field_data.reshape(
        field_data.shape[0],
        field_data.shape[1],
        field_data.shape[2],
        field_data.shape[3] // SLOTS,
        SLOTS,
    )


def cell_density(view_data):
    extent = (view_data.shape[1] - 2, view_data.shape[2] - 2, view_data.shape[3] - 2)
    center = view_data[:, 1:-1, 1:-1, 1:-1]
    summed = jnp.zeros(center.shape[1:], jnp.float32)
    for offset in cell_offsets:
        beside = shifted_cells(view_data, offset, extent)
        displace, weight, radius = pair_geometry(center, beside, offset)
        summed = summed + jnp.sum(weight * radial_density(radius), axis=-1)
    return summed


def cell_forces(view_data, slope_data):
    extent = (view_data.shape[1] - 2, view_data.shape[2] - 2, view_data.shape[3] - 2)
    center = view_data[:, 1:-1, 1:-1, 1:-1]
    slope_center = slope_data[0, 1:-1, 1:-1, 1:-1]
    force_sums = [jnp.zeros(center.shape[1:], jnp.float32) for component in range(3)]
    pair_sum = jnp.zeros(center.shape[1:], jnp.float32)
    for offset in cell_offsets:
        beside = shifted_cells(view_data, offset, extent)
        slope_beside = shifted_cells(slope_data, offset, extent)[0]
        displace, weight, radius = pair_geometry(center, beside, offset)
        pair_value, pair_slope, dens_value, dens_slope = pair_terms(radius)
        factor = (
            weight
            * (pair_slope + (slope_center[..., :, None] + slope_beside[..., None, :]) * dens_slope)
            / radius
        )
        force_sums = [
            force_sums[component] + jnp.sum(factor * displace[component], axis=-1)
            for component in range(3)
        ]
        pair_sum = pair_sum + jnp.sum(weight * pair_value, axis=-1)
    return (jnp.stack(force_sums), pair_sum)


def ghosts(field_data):
    along_z = with_halo(field_data, (("gz", 3),), SLOTS)
    return with_halo(along_z, (("gx", 1), ("gy", 2)), 1)


def on_device(positions, counts):
    cells_x, cells_y, cells_z = counts.shape
    occupied = (
        lax.broadcasted_iota(jnp.int32, (cells_x, cells_y, cells_z, SLOTS), 3) < counts[..., None]
    ).astype(jnp.float32)
    packed = jnp.concatenate(
        [positions, occupied.reshape(cells_x, cells_y, cells_z * SLOTS)[None]], axis=0
    )
    view_data = cell_view(ghosts(packed))
    density = cell_density(view_data)
    embed_value, embed_slope = embedding(density)
    slope = embed_slope * occupied
    slope_data = cell_view(ghosts(slope.reshape(1, cells_x, cells_y, cells_z * SLOTS)))
    forces, pair_sum = cell_forces(view_data, slope_data)
    energy = occupied * (embed_value + 0.5 * pair_sum)
    return (
        forces.reshape(3, cells_x, cells_y, cells_z * SLOTS),
        energy.reshape(cells_x, cells_y, cells_z * SLOTS),
    )


def solution(mesh):
    return jax.shard_map(
        on_device,
        mesh=mesh,
        in_specs=(P(None, "gx", "gy", "gz"), P("gx", "gy", "gz")),
        out_specs=(P(None, "gx", "gy", "gz"), P("gx", "gy", "gz")),
        check_vma=False,
    )
```

profile of v0, /device:TPU:24, one launch (start us, length us, event | category | flops | bytes accessed | tf_op | source)
XLA Modules:
  0.0 245.0 jit_solution(8374726925732736069)
XLA Ops:
  0.7 0.8 copy.7
  1.7 0.6 copy-done
  2.4 3.0 %collective-permute-start.1 = (f32[4,4,4,64]{3,2,1,0:T(4,128)S(1)}, f32[4,4,4,64]{3,2,1,0:T(4,128)S(1)}, u32[]{:S(2)}, u32[]{:S(2)}) collective-permute-start(f32[4,4,4,64]{3,2,1,0:T(4,128)S(1)} %get-tuple-element.337), channel_id=1, source_target_pairs={{1,0},{2,1},{3,2},{4,3},{5,4},{6,5},{7,6},{0,7},{9,8},{10,9},{11,1... | collective-permute-start | bytes 49160 | tf_op jit(solution)/shard_map/ppermute | solution.py:42
  5.4 1.6 collective-permute-done
  7.1 3.8 %collective-permute-start.2 = (f32[4,1,4,256]{3,2,1,0:T(4,128)S(1)}, f32[4,1,4,256]{3,2,1,0:T(4,128)S(1)}, u32[]{:S(2)}, u32[]{:S(2)}) collective-permute-start(f32[4,1,4,256]{3,2,1,0:T(4,128)S(1)} %get-tuple-element.305), channel_id=1, source_target_pairs={{0,32},{32,64},{64,96},{96,128},{128,160},{160,192},{192,224},{224... | collective-permute-start | bytes 49160 | tf_op jit(solution)/shard_map/ppermute | solution.py:41
  10.9 16.8 %collective-permute-start.3 = (f32[4,1,4,256]{3,2,1,0:T(4,128)S(1)}, f32[4,1,4,256]{3,2,1,0:T(4,128)S(1)}, u32[]{:S(2)}, u32[]{:S(2)}) collective-permute-start(f32[4,1,4,256]{3,2,1,0:T(4,128)S(1)} %get-tuple-element.306), channel_id=1, source_target_pairs={{32,0},{64,32},{96,64},{128,96},{160,128},{192,160},{224,192},{256... | collective-permute-start | bytes 49160 | tf_op jit(solution)/shard_map/ppermute | solution.py:42
  27.7 1.4 collective-permute-done.3
  29.1 0.2 pad_maximum_fusion.8
  29.3 2.1 collective-permute-start.4
  31.4 3.7 %collective-permute-start.5 = (f32[4,6,1,256]{3,2,1,0:T(1,128)S(1)}, f32[4,6,1,256]{3,2,1,0:T(1,128)S(1)}, u32[]{:S(2)}, u32[]{:S(2)}) collective-permute-start(f32[4,6,1,256]{3,2,1,0:T(1,128)S(1)} %get-tuple-element.304), channel_id=1, source_target_pairs={{8,0},{16,8},{24,16},{0,24},{9,1},{17,9},{25,17},{1,25},{10,2},{18... | collective-permute-start | bytes 73736 | tf_op jit(solution)/shard_map/ppermute | solution.py:42
  35.2 3.2 %collective-permute-done.5 = f32[4,6,1,256]{3,2,1,0:T(1,128)S(1)} collective-permute-done((f32[4,6,1,256]{3,2,1,0:T(1,128)S(1)}, f32[4,6,1,256]{3,2,1,0:T(1,128)S(1)}, u32[]{:S(2)}, u32[]{:S(2)}) %collective-permute-start.5) | collective-permute-done | bytes 24608 | tf_op jit(solution)/shard_map/ppermute | solution.py:42
  38.6 0.2 reshape.1949
  38.9 0.1 slice_bitcast_fusion.62
  39.0 0.1 fusion.1061
  39.3 0.2 fusion.1068
  39.5 0.1 fusion.1063
  39.6 4.6 %fusion.924 = (f32[4,4,2,64]{3,2,1,0:T(2,128)S(1)}, f32[4,4,2,64]{3,2,1,0:T(2,128)S(1)}, f32[4,4,2,64]{3,2,1,0:T(2,128)S(1)}) fusion(f32[4,4,2,64]{3,2,1,0:T(2,128)S(1)} %get-tuple-element.294, f32[4,4,2,64]{3,2,1,0:T(2,128)S(1)} %get-tuple-element.302, f32[4,4,2,64]{3,2,1,0:T(2,128)S(1)} %get-tuple-element.295, ...), kind=kLoop, calls=%fused_computation.1568 | loop fusion | flops 10217472 | bytes 155648 | tf_op jit(solution)/shard_map/reduce_sum | solution.py:172
  44.4 5.9 %fusion.954 = (f32[4,4,2,64]{3,2,1,0:T(2,128)S(1)}, f32[4,4,2,64]{3,2,1,0:T(2,128)S(1)}, f32[4,4,2,64]{3,2,1,0:T(2,128)S(1)}, f32[4,4,2,64]{3,2,1,0:T(2,128)S(1)}) fusion(f32[4,4,2,64]{3,2,1,0:T(2,128)S(1)} %get-tuple-element.237, f32[4,4,2,64]{3,2,1,0:T(2,128)S(1)} %get-tuple-element.302, f32[4,4,2,64]{3,2,1,0:T(2,128)S(1)} %get-tuple-element.295, ...), kind=kLoop, calls=%fused_computation.1598 | loop fusion | flops 13754368 | bytes 180224 | tf_op jit(solution)/shard_map/reduce_sum | solution.py:172
  50.6 4.6 %fusion.922 = (f32[4,4,2,64]{3,2,1,0:T(2,128)S(1)}, f32[4,4,2,64]{3,2,1,0:T(2,128)S(1)}, f32[4,4,2,64]{3,2,1,0:T(2,128)S(1)}) fusion(f32[4,4,2,64]{3,2,1,0:T(2,128)S(1)} %get-tuple-element.301, f32[4,4,2,64]{3,2,1,0:T(2,128)S(1)} %get-tuple-element.302, f32[4,4,2,64]{3,2,1,0:T(2,128)S(1)} %get-tuple-element.295, ...), kind=kLoop, calls=%fused_computation.1566 | loop fusion | flops 10217472 | bytes 155648 | tf_op jit(solution)/shard_map/reduce_sum | solution.py:172
  55.4 4.6 %fusion.926 = (f32[4,4,2,64]{3,2,1,0:T(2,128)S(1)}, f32[4,4,2,64]{3,2,1,0:T(2,128)S(1)}, f32[4,4,2,64]{3,2,1,0:T(2,128)S(1)}) fusion(f32[4,4,2,64]{3,2,1,0:T(2,128)S(1)} %get-tuple-element.290, f32[4,4,2,64]{3,2,1,0:T(2,128)S(1)} %get-tuple-element.302, f32[4,4,2,64]{3,2,1,0:T(2,128)S(1)} %get-tuple-element.295, ...), kind=kLoop, calls=%fused_computation.1570 | loop fusion | flops 10217472 | bytes 155648 | tf_op jit(solution)/shard_map/reduce_sum | solution.py:172
  60.2 4.6 %fusion.928 = (f32[4,4,2,64]{3,2,1,0:T(2,128)S(1)}, f32[4,4,2,64]{3,2,1,0:T(2,128)S(1)}, f32[4,4,2,64]{3,2,1,0:T(2,128)S(1)}) fusion(f32[4,4,2,64]{3,2,1,0:T(2,128)S(1)} %get-tuple-element.286, f32[4,4,2,64]{3,2,1,0:T(2,128)S(1)} %get-tuple-element.302, f32[4,4,2,64]{3,2,1,0:T(2,128)S(1)} %get-tuple-element.295, ...), kind=kLoop, calls=%fused_computation.1572 | loop fusion | flops 10217472 | bytes 155648 | tf_op jit(solution)/shard_map/reduce_sum | solution.py:172
  64.9 3.3 %fusion.936 = (f32[4,4,2,64]{3,2,1,0:T(2,128)S(1)}, f32[4,4,2,64]{3,2,1,0:T(2,128)S(1)}) fusion(f32[4,4,2,64]{3,2,1,0:T(2,128)S(1)} %get-tuple-element.270, f32[4,4,2,64]{3,2,1,0:T(2,128)S(1)} %get-tuple-element.302, f32[4,4,2,64]{3,2,1,0:T(2,128)S(1)} %get-tuple-element.295, f32[4,4,2,64]{3,2,1,0:T(2,128)S(1)} %get-tuple-element.267, ...), kind=kLoop, calls=%fused_computation.1580 | loop fusion | flops 6811648 | bytes 114688 | tf_op jit(solution)/shard_map/reduce_sum | solution.py:172
  68.2 4.6 %fusion.934 = (f32[4,4,2,64]{3,2,1,0:T(2,128)S(1)}, f32[4,4,2,64]{3,2,1,0:T(2,128)S(1)}, f32[4,4,2,64]{3,2,1,0:T(2,128)S(1)}) fusion(f32[4,4,2,64]{3,2,1,0:T(2,128)S(1)} %get-tuple-element.274, f32[4,4,2,64]{3,2,1,0:T(2,128)S(1)} %get-tuple-element.302, f32[4,4,2,64]{3,2,1,0:T(2,128)S(1)} %get-tuple-element.295, ...), kind=kLoop, calls=%fused_computation.1578 | loop fusion | flops 10217472 | bytes 155648 | tf_op jit(solution)/shard_map/reduce_sum | solution.py:172
  72.8 4.6 %fusion.932 = (f32[4,4,2,64]{3,2,1,0:T(2,128)S(1)}, f32[4,4,2,64]{3,2,1,0:T(2,128)S(1)}, f32[4,4,2,64]{3,2,1,0:T(2,128)S(1)}) fusion(f32[4,4,2,64]{3,2,1,0:T(2,128)S(1)} %get-tuple-element.278, f32[4,4,2,64]{3,2,1,0:T(2,128)S(1)} %get-tuple-element.302, f32[4,4,2,64]{3,2,1,0:T(2,128)S(1)} %get-tuple-element.295, ...), kind=kLoop, calls=%fused_computation.1576 | loop fusion | flops 10217472 | bytes 155648 | tf_op jit(solution)/shard_map/reduce_sum | solution.py:172
  77.5 4.6 %fusion.930 = (f32[4,4,2,64]{3,2,1,0:T(2,128)S(1)}, f32[4,4,2,64]{3,2,1,0:T(2,128)S(1)}, f32[4,4,2,64]{3,2,1,0:T(2,128)S(1)}) fusion(f32[4,4,2,64]{3,2,1,0:T(2,128)S(1)} %get-tuple-element.282, f32[4,4,2,64]{3,2,1,0:T(2,128)S(1)} %get-tuple-element.302, f32[4,4,2,64]{3,2,1,0:T(2,128)S(1)} %get-tuple-element.295, ...), kind=kLoop, calls=%fused_computation.1574 | loop fusion | flops 10217472 | bytes 155648 | tf_op jit(solution)/shard_map/reduce_sum | solution.py:172
  82.3 3.0 %collective-permute-start.7 = (f32[1,4,4,64]{3,2,1,0:T(4,128)S(1)}, f32[1,4,4,64]{3,2,1,0:T(4,128)S(1)}, u32[]{:S(2)}, u32[]{:S(2)}) collective-permute-start(f32[1,4,4,64]{3,2,1,0:T(4,128)S(1)} %get-tuple-element.341), channel_id=1, source_target_pairs={{1,0},{2,1},{3,2},{4,3},{5,4},{6,5},{7,6},{0,7},{9,8},{10,9},{11,1... | collective-permute-start | bytes 12296 | tf_op jit(solution)/shard_map/ppermute | solution.py:42
  85.3 1.3 collective-permute-done.6
  86.7 1.9 collective-permute-start.8
  88.6 5.4 %collective-permute-start.9 = (f32[1,1,4,256]{3,2,1,0:T(4,128)S(1)}, f32[1,1,4,256]{3,2,1,0:T(4,128)S(1)}, u32[]{:S(2)}, u32[]{:S(2)}) collective-permute-start(f32[1,1,4,256]{3,2,1,0:T(4,128)S(1)} %get-tuple-element.339), channel_id=1, source_target_pairs={{32,0},{64,32},{96,64},{128,96},{160,128},{192,160},{224,192},{256... | collective-permute-start | bytes 12296 | tf_op jit(solution)/shard_map/ppermute | solution.py:42
  94.1 1.3 collective-permute-done.9
  95.5 2.3 collective-permute-start.10
  97.8 3.6 %collective-permute-start.11 = (f32[1,6,1,256]{3,2,1,0:T(1,128)S(1)}, f32[1,6,1,256]{3,2,1,0:T(1,128)S(1)}, u32[]{:S(2)}, u32[]{:S(2)}) collective-permute-start(f32[1,6,1,256]{3,2,1,0:T(1,128)S(1)} %get-tuple-element.335), channel_id=1, source_target_pairs={{8,0},{16,8},{24,16},{0,24},{9,1},{17,9},{25,17},{1,25},{10,2},{18... | collective-permute-start | bytes 18440 | tf_op jit(solution)/shard_map/ppermute | solution.py:42
  102.4 2.1 collective-permute-done.11
  104.8 10.2 %fusion.314 = (f32[4,4,2,64]{3,2,1,0:T(2,128)S(1)}, f32[4,4,2,64]{3,2,1,0:T(2,128)S(1)}, f32[4,4,2,64]{3,2,1,0:T(2,128)S(1)}, f32[4,4,2,64]{3,2,1,0:T(2,128)S(1)...) fusion(f32[4,4,2,64]{3,2,1,0:T(2,128)S(1)} %get-tuple-element.2, ...), kind=kLoop, calls=%fused_computation.958 | loop fusion | flops 25411584 | bytes 188416 | tf_op jit(solution)/shard_map/reduce_sum | solution.py:193
  115.1 10.0 %fusion.290 = (f32[4,4,2,64]{3,2,1,0:T(2,128)S(1)}, f32[4,4,2,64]{3,2,1,0:T(2,128)S(1)}, f32[4,4,2,64]{3,2,1,0:T(2,128)S(1)}, f32[4,4,2,64]{3,2,1,0:T(2,128)S(1)...) fusion(f32[4,4,2,64]{3,2,1,0:T(2,128)S(1)} %get-tuple-element.2, ...), kind=kLoop, calls=%fused_computation.934 | loop fusion | flops 25411584 | bytes 188416 | tf_op jit(solution)/shard_map/reduce_sum | solution.py:193
  125.3 10.0 %fusion.266 = (f32[4,4,2,64]{3,2,1,0:T(2,128)S(1)}, f32[4,4,2,64]{3,2,1,0:T(2,128)S(1)}, f32[4,4,2,64]{3,2,1,0:T(2,128)S(1)}, f32[4,4,2,64]{3,2,1,0:T(2,128)S(1)...) fusion(f32[4,4,2,64]{3,2,1,0:T(2,128)S(1)} %get-tuple-element.2, ...), kind=kLoop, calls=%fused_computation.910 | loop fusion | flops 25411584 | bytes 188416 | tf_op jit(solution)/shard_map/reduce_sum | solution.py:193
  135.4 10.0 %fusion.242 = (f32[4,4,2,64]{3,2,1,0:T(2,128)S(1)}, f32[4,4,2,64]{3,2,1,0:T(2,128)S(1)}, f32[4,4,2,64]{3,2,1,0:T(2,128)S(1)}, f32[4,4,2,64]{3,2,1,0:T(2,128)S(1)...) fusion(f32[4,4,2,64]{3,2,1,0:T(2,128)S(1)} %get-tuple-element.2, ...), kind=kLoop, calls=%fused_computation.886 | loop fusion | flops 25411584 | bytes 188416 | tf_op jit(solution)/shard_map/reduce_sum | solution.py:193
  145.5 10.0 %fusion.110 = (f32[4,4,2,64]{3,2,1,0:T(2,128)S(1)}, f32[4,4,2,64]{3,2,1,0:T(2,128)S(1)}, f32[4,4,2,64]{3,2,1,0:T(2,128)S(1)}, f32[4,4,2,64]{3,2,1,0:T(2,128)S(1)...) fusion(f32[4,4,2,64]{3,2,1,0:T(2,128)S(1)} %get-tuple-element.2, ...), kind=kLoop, calls=%fused_computation.754 | loop fusion | flops 25411584 | bytes 188416 | tf_op jit(solution)/shard_map/reduce_sum | solution.py:193
  155.6 10.0 %fusion.86 = (f32[4,4,2,64]{3,2,1,0:T(2,128)S(1)}, f32[4,4,2,64]{3,2,1,0:T(2,128)S(1)}, f32[4,4,2,64]{3,2,1,0:T(2,128)S(1)}, f32[4,4,2,64]{3,2,1,0:T(2,128)S(1)}...) fusion(f32[4,4,2,64]{3,2,1,0:T(2,128)S(1)} %get-tuple-element.2, ...), kind=kLoop, calls=%fused_computation.730 | loop fusion | flops 25411584 | bytes 188416 | tf_op jit(solution)/shard_map/reduce_sum | solution.py:193
  165.6 10.0 %fusion.62 = (f32[4,4,2,64]{3,2,1,0:T(2,128)S(1)}, f32[4,4,2,64]{3,2,1,0:T(2,128)S(1)}, f32[4,4,2,64]{3,2,1,0:T(2,128)S(1)}, f32[4,4,2,64]{3,2,1,0:T(2,128)S(1)}...) fusion(f32[4,4,2,64]{3,2,1,0:T(2,128)S(1)} %get-tuple-element.2, ...), kind=kLoop, calls=%fused_computation.706 | loop fusion | flops 25411584 | bytes 188416 | tf_op jit(solution)/shard_map/reduce_sum | solution.py:193
  175.7 10.0 %fusion.4 = (f32[4,4,2,64]{3,2,1,0:T(2,128)S(1)}, f32[4,4,2,64]{3,2,1,0:T(2,128)S(1)}, f32[4,4,2,64]{3,2,1,0:T(2,128)S(1)}, f32[4,4,2,64]{3,2,1,0:T(2,128)S(1)},...) fusion(f32[4,4,2,64]{3,2,1,0:T(2,128)S(1)} %get-tuple-element.2, ...), kind=kLoop, calls=%fused_computation.648 | loop fusion | flops 25411584 | bytes 188416 | tf_op jit(solution)/shard_map/reduce_sum | solution.py:193
  185.7 10.3 %fusion.218 = (f32[4,4,2,64]{3,2,1,0:T(2,128)S(1)}, f32[4,4,2,64]{3,2,1,0:T(2,128)S(1)}, f32[4,4,2,64]{3,2,1,0:T(2,128)S(1)}, f32[4,4,2,64]{3,2,1,0:T(2,128)S(1)...) fusion(f32[4,4,2,64]{3,2,1,0:T(2,128)S(1)} %get-tuple-element.2, ...), kind=kLoop, calls=%fused_computation.862 | loop fusion | flops 25411584 | bytes 188416 | tf_op jit(solution)/shard_map/reduce_sum | solution.py:193
  196.0 10.0 %fusion.194 = (f32[4,4,2,64]{3,2,1,0:T(2,128)S(1)}, f32[4,4,2,64]{3,2,1,0:T(2,128)S(1)}, f32[4,4,2,64]{3,2,1,0:T(2,128)S(1)}, f32[4,4,2,64]{3,2,1,0:T(2,128)S(1)...) fusion(f32[4,4,2,64]{3,2,1,0:T(2,128)S(1)} %get-tuple-element.2, ...), kind=kLoop, calls=%fused_computation.838 | loop fusion | flops 25411584 | bytes 188416 | tf_op jit(solution)/shard_map/reduce_sum | solution.py:193
  206.0 10.0 %fusion.158 = (f32[4,4,2,64]{3,2,1,0:T(2,128)S(1)}, f32[4,4,2,64]{3,2,1,0:T(2,128)S(1)}, f32[4,4,2,64]{3,2,1,0:T(2,128)S(1)}, f32[4,4,2,64]{3,2,1,0:T(2,128)S(1)...) fusion(f32[4,4,2,64]{3,2,1,0:T(2,128)S(1)} %get-tuple-element.2, ...), kind=kLoop, calls=%fused_computation.802 | loop fusion | flops 25411584 | bytes 188416 | tf_op jit(solution)/shard_map/reduce_sum | solution.py:193
  216.1 10.0 %fusion.134 = (f32[4,4,2,64]{3,2,1,0:T(2,128)S(1)}, f32[4,4,2,64]{3,2,1,0:T(2,128)S(1)}, f32[4,4,2,64]{3,2,1,0:T(2,128)S(1)}, f32[4,4,2,64]{3,2,1,0:T(2,128)S(1)...) fusion(f32[4,4,2,64]{3,2,1,0:T(2,128)S(1)} %get-tuple-element.2, ...), kind=kLoop, calls=%fused_computation.778 | loop fusion | flops 25411584 | bytes 188416 | tf_op jit(solution)/shard_map/reduce_sum | solution.py:193
  226.1 13.9 %fusion.182 = (f32[4,4,2,64]{3,2,1,0:T(2,128)S(1)}, f32[4,4,2,64]{3,2,1,0:T(2,128)S(1)}, f32[4,4,2,64]{3,2,1,0:T(2,128)S(1)}, f32[4,4,2,64]{3,2,1,0:T(2,128)S(1)...) fusion(f32[4,4,2,64]{3,2,1,0:T(2,128)S(1)} %get-tuple-element.2, ...), kind=kLoop, calls=%fused_computation.826 | loop fusion | flops 38248448 | bytes 237568 | tf_op jit(solution)/shard_map/reduce_sum | solution.py:193
  243.7 0.6 pad_maximum_fusion.9
  244.3 0.6 fusion.1104
  (104 shorter events, 7.5 us)
Async XLA Ops:
  1.6 0.7 copy-start
  2.4 4.6 %collective-permute-start = (f32[4,4,4,64]{3,2,1,0:T(4,128)S(1)}, f32[4,4,4,64]{3,2,1,0:T(4,128)S(1)}, u32[]{:S(2)}, u32[]{:S(2)}) collective-permute-start(f32[4,4,4,64]{3,2,1,0:T(4,128)S(1)} %get-tuple-element.336), channel_id=1, source_target_pairs={{0,1},{1,2},{2,3},{3,4},{4,5},{5,6},{6,7},{7,0},{8,9},{9,10},{10,1... | collective-permute-start | bytes 49160 | tf_op jit(solution)/shard_map/ppermute | solution.py:41
  2.4 4.6 %collective-permute-start.1 = (f32[4,4,4,64]{3,2,1,0:T(4,128)S(1)}, f32[4,4,4,64]{3,2,1,0:T(4,128)S(1)}, u32[]{:S(2)}, u32[]{:S(2)}) collective-permute-start(f32[4,4,4,64]{3,2,1,0:T(4,128)S(1)} %get-tuple-element.337), channel_id=1, source_target_pairs={{1,0},{2,1},{3,2},{4,3},{5,4},{6,5},{7,6},{0,7},{9,8},{10,9},{11,1... | collective-permute-start | bytes 49160 | tf_op jit(solution)/shard_map/ppermute | solution.py:42
  7.1 20.6 %collective-permute-start.2 = (f32[4,1,4,256]{3,2,1,0:T(4,128)S(1)}, f32[4,1,4,256]{3,2,1,0:T(4,128)S(1)}, u32[]{:S(2)}, u32[]{:S(2)}) collective-permute-start(f32[4,1,4,256]{3,2,1,0:T(4,128)S(1)} %get-tuple-element.305), channel_id=1, source_target_pairs={{0,32},{32,64},{64,96},{96,128},{128,160},{160,192},{192,224},{224... | collective-permute-start | bytes 49160 | tf_op jit(solution)/shard_map/ppermute | solution.py:41
  10.9 18.2 %collective-permute-start.3 = (f32[4,1,4,256]{3,2,1,0:T(4,128)S(1)}, f32[4,1,4,256]{3,2,1,0:T(4,128)S(1)}, u32[]{:S(2)}, u32[]{:S(2)}) collective-permute-start(f32[4,1,4,256]{3,2,1,0:T(4,128)S(1)} %get-tuple-element.306), channel_id=1, source_target_pairs={{32,0},{64,32},{96,64},{128,96},{160,128},{192,160},{224,192},{256... | collective-permute-start | bytes 49160 | tf_op jit(solution)/shard_map/ppermute | solution.py:42
  29.3 5.9 %collective-permute-start.4 = (f32[4,6,1,256]{3,2,1,0:T(1,128)S(1)}, f32[4,6,1,256]{3,2,1,0:T(1,128)S(1)}, u32[]{:S(2)}, u32[]{:S(2)}) collective-permute-start(f32[4,6,1,256]{3,2,1,0:T(1,128)S(1)} %get-tuple-element.303), channel_id=1, source_target_pairs={{0,8},{8,16},{16,24},{24,0},{1,9},{9,17},{17,25},{25,1},{2,10},{10... | collective-permute-start | bytes 73736 | tf_op jit(solution)/shard_map/ppermute | solution.py:41
  31.4 6.9 %collective-permute-start.5 = (f32[4,6,1,256]{3,2,1,0:T(1,128)S(1)}, f32[4,6,1,256]{3,2,1,0:T(1,128)S(1)}, u32[]{:S(2)}, u32[]{:S(2)}) collective-permute-start(f32[4,6,1,256]{3,2,1,0:T(1,128)S(1)} %get-tuple-element.304), channel_id=1, source_target_pairs={{8,0},{16,8},{24,16},{0,24},{9,1},{17,9},{25,17},{1,25},{10,2},{18... | collective-permute-start | bytes 73736 | tf_op jit(solution)/shard_map/ppermute | solution.py:42
  82.3 4.3 %collective-permute-start.6 = (f32[1,4,4,64]{3,2,1,0:T(4,128)S(1)}, f32[1,4,4,64]{3,2,1,0:T(4,128)S(1)}, u32[]{:S(2)}, u32[]{:S(2)}) collective-permute-start(f32[1,4,4,64]{3,2,1,0:T(4,128)S(1)} %get-tuple-element.340), channel_id=1, source_target_pairs={{0,1},{1,2},{2,3},{3,4},{4,5},{5,6},{6,7},{7,0},{8,9},{9,10},{10,1... | collective-permute-start | bytes 12296 | tf_op jit(solution)/shard_map/ppermute | solution.py:41
  82.3 4.3 %collective-permute-start.7 = (f32[1,4,4,64]{3,2,1,0:T(4,128)S(1)}, f32[1,4,4,64]{3,2,1,0:T(4,128)S(1)}, u32[]{:S(2)}, u32[]{:S(2)}) collective-permute-start(f32[1,4,4,64]{3,2,1,0:T(4,128)S(1)} %get-tuple-element.341), channel_id=1, source_target_pairs={{1,0},{2,1},{3,2},{4,3},{5,4},{6,5},{7,6},{0,7},{9,8},{10,9},{11,1... | collective-permute-start | bytes 12296 | tf_op jit(solution)/shard_map/ppermute | solution.py:42
  86.7 7.3 %collective-permute-start.8 = (f32[1,1,4,256]{3,2,1,0:T(4,128)S(1)}, f32[1,1,4,256]{3,2,1,0:T(4,128)S(1)}, u32[]{:S(2)}, u32[]{:S(2)}) collective-permute-start(f32[1,1,4,256]{3,2,1,0:T(4,128)S(1)} %get-tuple-element.338), channel_id=1, source_target_pairs={{0,32},{32,64},{64,96},{96,128},{128,160},{160,192},{192,224},{224... | collective-permute-start | bytes 12296 | tf_op jit(solution)/shard_map/ppermute | solution.py:41
  88.6 6.7 %collective-permute-start.9 = (f32[1,1,4,256]{3,2,1,0:T(4,128)S(1)}, f32[1,1,4,256]{3,2,1,0:T(4,128)S(1)}, u32[]{:S(2)}, u32[]{:S(2)}) collective-permute-start(f32[1,1,4,256]{3,2,1,0:T(4,128)S(1)} %get-tuple-element.339), channel_id=1, source_target_pairs={{32,0},{64,32},{96,64},{128,96},{160,128},{192,160},{224,192},{256... | collective-permute-start | bytes 12296 | tf_op jit(solution)/shard_map/ppermute | solution.py:42
  95.5 6.9 %collective-permute-start.10 = (f32[1,6,1,256]{3,2,1,0:T(1,128)S(1)}, f32[1,6,1,256]{3,2,1,0:T(1,128)S(1)}, u32[]{:S(2)}, u32[]{:S(2)}) collective-permute-start(f32[1,6,1,256]{3,2,1,0:T(1,128)S(1)} %get-tuple-element.334), channel_id=1, source_target_pairs={{0,8},{8,16},{16,24},{24,0},{1,9},{9,17},{17,25},{25,1},{2,10},{10... | collective-permute-start | bytes 18440 | tf_op jit(solution)/shard_map/ppermute | solution.py:41
  97.8 6.7 %collective-permute-start.11 = (f32[1,6,1,256]{3,2,1,0:T(1,128)S(1)}, f32[1,6,1,256]{3,2,1,0:T(1,128)S(1)}, u32[]{:S(2)}, u32[]{:S(2)}) collective-permute-start(f32[1,6,1,256]{3,2,1,0:T(1,128)S(1)} %get-tuple-element.335), channel_id=1, source_target_pairs={{8,0},{16,8},{24,16},{0,24},{9,1},{17,9},{25,17},{1,25},{10,2},{18... | collective-permute-start | bytes 18440 | tf_op jit(solution)/shard_map/ppermute | solution.py:42
where the time goes:
time: 245 us
  other arithmetic  179 us (73%)
  starting transfers between devices  45.5 us (19%)
  waiting for transfers between devices  11 us (4%)
  local copies, waits for them, and re-layouts  8.04 us (3%)
    reduce_sum x13, other arithmetic, cell_forces(): jnp.sum(factor * displace[component], axis=-1)  135 us
    reduce_sum x9, other arithmetic, cell_density(): summed = summed + jnp.sum(weight * radial_density(radius), axis=-1)  41.5 us
    ppermute x6, starting transfers between devices, with_halo(): after = lax.ppermute(first, axis, down)  35.4 us
    ppermute x6, starting transfers between devices, with_halo(): before = lax.ppermute(last, axis, up)  10.1 us
    ppermute x6, waiting for transfers between devices, with_halo(): after = lax.ppermute(first, axis, down)  8.04 us
  transfers between devices with their start and end apart: 12, of which 6 were waited for; matrix products, arithmetic and copies ran while one was open for 0% of the time, Pallas kernels for 0%

commit v1 on v0

v1 whole, which is shorter than its diff:
```python
import functools

import jax
import jax.numpy as jnp
import numpy as np
from jax import lax
from jax.experimental import pallas as pl
from jax.experimental.pallas import tpu as pltpu
from jax.sharding import PartitionSpec as P

SLOTS = 64
lattice_const = 3.615
SPAN_XY = 2.0 * lattice_const
SPAN_Z = 4.0 * lattice_const
cut_radius = 5.50679
cut_width = 0.50037
dens_scale = 3.80362
beta_one = 0.17394
radius_three = -2.19885
energy_one = 201.458
energy_two = 0.00659288
radius_one = 0.83591
radius_two = 4.46867
alpha_one = 2.97758
alpha_two = 1.54927
shift_delta = 0.0086225
repulsion = ((4.0, 2.24), (40.0, 1.8), (1150.0, 1.2))
embed_zero = -2.28235
embed_curve = 1.35535
lower_terms = (-1.27775, -0.86074, 1.78804, 2.97571)
upper_quartic = 0.4
upper_damping = 0.3
LOG2E = 1.4426950408889634

HB = 1.836
ZOFF = 0.228
NB = 28
CAP = 8
MAIN = NB * CAP
NSLOT = 512
NCHUNK = NSLOT // 8
FAR = 1000.0


def index_tables():
    lane = np.arange(128)
    sub = np.arange(8)[:, None]
    unit = lane // 8
    used = np.minimum(unit, 11)
    dens = []
    for row in range(7):
        for dy in (-1, 0, 1):
            col = (row + used // 6) * 8 + (used % 6 + 1 + dy)
            dens.append(np.broadcast_to(col, (8, 128)))
    back, mask = [], []
    for t in range(3):
        x, y = lane // 8 - 1, lane % 8 - 1
        ok = (lane < 64) & (x >= 2 * t) & (x < 2 * t + 2) & (y >= 0) & (y < 6)
        src = np.where(ok, ((x - 2 * t) * 6 + y) * 8, 0) + sub
        back.append(src)
        mask.append(np.broadcast_to(ok.astype(np.int32), (8, 128)))
    forc = []
    for dx in (-1, 0, 1):
        for dy in (-1, 0, 1):
            col = (unit // 4 + 2 + dx) * 8 + (unit % 4 + 2 + dy)
            forc.append(np.broadcast_to(col, (8, 128)))
    fback = np.where(lane < 16, lane * 8, 0) + sub
    tabs = np.stack(dens + back + mask + forc + [fback]).astype(np.int32)
    return tabs


T_DENS, T_BACK, T_MASK, T_FORC, T_FBACK = 0, 21, 24, 27, 36


def split3(v):
    hi = v.astype(jnp.bfloat16).astype(jnp.float32)
    rest = v - hi
    mid = rest.astype(jnp.bfloat16).astype(jnp.float32)
    return hi, mid, rest - mid


def embedding(density):
    e = density - 1.0
    e2 = e * e
    e3 = e2 * e
    l0, l1, l2, l3 = lower_terms
    low = embed_zero + e2 * (0.5 * embed_curve + e * (l0 + e * (l1 + e * (l2 + e * l3))))
    lows = e * (embed_curve + e * (3.0 * l0 + e * (4.0 * l1 + e * (5.0 * l2 + e * (6.0 * l3)))))
    num = embed_zero + e2 * (0.5 * embed_curve + e * (l0 + e * upper_quartic))
    nums = e * (embed_curve + e * (3.0 * l0 + e * (4.0 * upper_quartic)))
    below = e < 0.0
    den = jnp.where(below, 1.0, 1.0 + upper_damping * e3)
    inv = 1.0 / den
    up = num * inv
    ups = (nums * den - num * (3.0 * upper_damping) * e2) * inv * inv
    return jnp.where(below, low, up), jnp.where(below, lows, ups)


def geometry(xi, yi, zi, xj, yj, zj, mask_self):
    dx, dy, dz = xj - xi, yj - yi, zj - zi
    r2 = dx * dx + dy * dy + dz * dz
    if mask_self:
        r2 = jnp.where(r2 < 0.25, 100.0, r2)
    rinv = lax.rsqrt(r2)
    return dx, dy, dz, rinv, r2 * rinv


def rho_tile(xi, yi, zi, xj, yj, zj, mask_self):
    _, _, _, _, r = geometry(xi, yi, zi, xj, yj, zj, mask_self)
    t = jnp.minimum(r * (1.0 / cut_width) - cut_radius / cut_width, 0.0)
    t2 = t * t
    q = t2 * t2
    rs = r - radius_three
    ex = rs * (rs * (-beta_one * LOG2E)) + float(np.log2(dens_scale))
    return jnp.exp2(ex) * (q / (1.0 + q))


def force_tile(xi, yi, zi, si, xj, yj, zj, sj, mask_self):
    dx, dy, dz, rinv, r = geometry(xi, yi, zi, xj, yj, zj, mask_self)
    t = jnp.minimum(r * (1.0 / cut_width) - cut_radius / cut_width, 0.0)
    t2 = t * t
    q = t2 * t2
    inv = 1.0 / (1.0 + q)
    taper = q * inv
    tslope = (t * t2) * (inv * inv) * (4.0 / cut_width)
    rs = r - radius_three
    gr = rs * (-beta_one * LOG2E)
    g = jnp.exp2(rs * gr + float(np.log2(dens_scale)))
    dslope = g * (gr * taper * (2.0 / LOG2E) + tslope)
    u1 = jnp.exp2(r * (-alpha_one * LOG2E) + alpha_one * LOG2E * radius_one)
    u2 = jnp.exp2(r * (-alpha_two * LOG2E) + alpha_two * LOG2E * radius_two)
    y1 = u1 * (u1 - 1.0)
    y2 = u2 * (u2 - 1.0)
    base = (y1 - u1) * energy_one + ((y2 - u2) * energy_two + shift_delta)
    bslope = y1 * (-2.0 * alpha_one * energy_one) + y2 * (-2.0 * alpha_two * energy_two)
    pval = base * taper
    pslope = bslope * taper + base * tslope
    rep = None
    for strength, reach in repulsion:
        s = jnp.maximum(reach - r, 0.0)
        g3 = (s * s) * (s * (4.0 * strength))
        pslope = pslope + g3
        rep = g3 * s if rep is None else rep + g3 * s
    pval = pval - 0.25 * rep
    f = (pslope + (si + sj) * dslope) * rinv
    return f * dx, f * dy, f * dz, pval


def kernel(h_ref, u_ref, tab_ref, force_ref, energy_ref,
           dest_ref, tc_ref, tx_ref, rho_ref, sl_ref, em_ref, jd_ref, jf_ref, tf_ref):
    f32 = jnp.float32
    row = lax.broadcasted_iota(jnp.int32, (64, 256), 0)
    lane = lax.broadcasted_iota(jnp.int32, (64, 256), 1)
    xa = h_ref[0] + (row // 8 - 2).astype(f32) * SPAN_XY
    ya = h_ref[1] + (row % 8 - 2).astype(f32) * SPAN_XY
    za = h_ref[2] + (lane // 64 - 1).astype(f32) * SPAN_Z
    fb = jnp.floor((za + (ZOFF + 6 * HB)) * (1.0 / HB))
    valid = (fb >= 0.0) & (fb < float(NB))
    bins = jnp.where(valid, fb, -1.0)

    biota = lax.broadcasted_iota(jnp.int32, (32, 256), 0).astype(f32)
    upper = u_ref[...]
    ranks = []
    for c in range(64):
        ob = jnp.where(bins[c : c + 1, :] == biota, 1.0, 0.0)
        pr = jnp.dot(ob, upper, preferred_element_type=f32)
        ranks.append(jnp.sum(ob * pr, axis=0, keepdims=True))
    rank = jnp.concatenate(ranks, axis=0)
    over = valid & (rank >= float(CAP))
    overf = jnp.where(over, 1.0, 0.0)
    orank = jnp.dot(overf, upper, preferred_element_type=f32)
    novf = jnp.max(jnp.where(over, orank + 1.0, 0.0)).astype(jnp.int32)
    nch = (novf + 7) // 8
    dest = jnp.where(over, orank + float(MAIN), bins * float(CAP) + rank)
    dest_ref[...] = jnp.where(valid, dest, -1.0)

    tc_ref[...] = jnp.zeros_like(tc_ref)
    pos = [split3(v) for v in (xa, ya, za)]
    ones = jnp.where(valid, 1.0, 0.0)
    siota = lax.broadcasted_iota(jnp.int32, (256, 256), 0).astype(f32)
    sub8 = lax.broadcasted_iota(jnp.int32, (8, 256), 0)

    def scatter(half):
        for g in range(8):
            parts = [p[8 * g : 8 * g + 8] for trio in pos for p in trio] + [ones[8 * g : 8 * g + 8]]
            acc = None
            for u in range(8):
                lhs = jnp.concatenate([jnp.where(sub8 == u, p, 0.0) for p in parts], axis=0)
                drow = dest_ref[8 * g + u : 8 * g + u + 1, :] - float(256 * half)
                oh = jnp.where(siota == drow, 1.0, 0.0)
                out = lax.dot_general(lhs, oh, (((1,), (1,)), ((), ())), preferred_element_type=f32)
                acc = out if acc is None else acc + out
            have = acc[72:80] > 0.5
            for k in range(3):
                v = acc[24 * k : 24 * k + 8] + acc[24 * k + 8 : 24 * k + 16] + acc[24 * k + 16 : 24 * k + 24]
                tc_ref[k, 8 * g : 8 * g + 8, 256 * half : 256 * half + 256] = jnp.where(have, v, FAR)

    scatter(0)

    @pl.when(nch > 4)
    def _():
        scatter(1)

    for k in range(3):
        tx_ref[k, 0:256, :] = tc_ref[k, :, 0:256].T

    @pl.when(nch > 4)
    def _():
        for k in range(3):
            tx_ref[k, 256:512, :] = tc_ref[k, :, 256:512].T

    def take(values, idx):
        return jnp.take_along_axis(values, idx, axis=1, mode="promise_in_bounds")

    def expand_dens(m):
        m8 = pl.multiple_of(m * 8, 8)
        vals = [tx_ref[k, pl.ds(m8, 8), :] for k in range(3)]
        for w in range(21):
            idx = tab_ref[T_DENS + w]
            for k in range(3):
                jd_ref[k, w, pl.ds(m8, 8), :] = take(vals[k], idx)

    pl.loop(0, NB + nch)(expand_dens)

    sub = lax.broadcasted_iota(jnp.int32, (8, 128), 0)
    lane128 = lax.broadcasted_iota(jnp.int32, (8, 128), 1)
    diag = sub == lane128 % 8

    def spread(v):
        return jnp.broadcast_to(jnp.sum(jnp.where(diag, v, 0.0), axis=0, keepdims=True), (8, 128))

    def total(v):
        return jnp.broadcast_to(jnp.sum(v, axis=0, keepdims=True), (8, 128))

    rho_ref[...] = jnp.ones_like(rho_ref)

    def dens_i(t, ic):
        i8 = pl.multiple_of(ic * 8, 8)
        xi, yi, zi = [spread(jd_ref[k, (2 * t + 1) * 3 + 1, pl.ds(i8, 8), :]) for k in range(3)]
        return jnp.where(xi > 0.5 * FAR, -FAR, xi), yi, zi

    def dens_j(acc, it, t, jc, count):
        for m in range(count):
            j8 = pl.multiple_of((jc + m) * 8, 8)
            for dx in range(3):
                for dy in range(3):
                    w = (2 * t + dx) * 3 + dy
                    xj, yj, zj = [jd_ref[k, w, pl.ds(j8, 8), :] for k in range(3)]
                    acc = acc + rho_tile(*it, xj, yj, zj, dx == 1 and dy == 1)
        return acc

    def dens_store(acc, t, ic):
        i8 = pl.multiple_of(ic * 8, 8)
        got = take(total(acc), tab_ref[T_BACK + t])
        rho_ref[pl.ds(i8, 8), :] = jnp.where(tab_ref[T_MASK + t] > 0, got, rho_ref[pl.ds(i8, 8), :])

    zero = jnp.zeros((8, 128), f32)

    def dens_main(n):
        e, t = n // 3, n % 3
        ic = e + 3
        it = dens_i(t, ic)
        acc = dens_j(zero, it, t, e, 7)
        acc = dens_j(acc, it, t, NB, 1)
        acc = lax.fori_loop(1, nch, lambda q, a: dens_j(a, it, t, NB + q, 1), acc)
        dens_store(acc, t, ic)

    @pl.when(nch == 0)
    def _():
        for w in range(21):
            for k in range(3):
                jd_ref[k, w, MAIN : MAIN + 8, :] = jnp.full((8, 128), FAR, f32)

    pl.loop(0, 66)(dens_main)

    def dens_over(n):
        q, t = n // 3, n % 3
        ic = NB + q
        it = dens_i(t, ic)
        acc = lax.fori_loop(0, 4, lambda g, a: dens_j(a, it, t, 7 * g, 7), zero)
        acc = lax.fori_loop(0, nch, lambda p, a: dens_j(a, it, t, NB + p, 1), acc)
        dens_store(acc, t, ic)

    pl.loop(0, 3 * nch)(dens_over)

    def embed_rows(start, size):
        occ = tx_ref[0, pl.ds(start, size), :] < 0.5 * FAR
        val, slo = embedding(rho_ref[pl.ds(start, size), :])
        em_ref[pl.ds(start, size), :] = jnp.where(occ, val, 0.0)
        sl_ref[pl.ds(start, size), :] = jnp.where(occ, slo, 0.0)

    embed_rows(0, 256)

    @pl.when(nch > 4)
    def _():
        embed_rows(256, 256)

    def expand_forc(m):
        m8 = pl.multiple_of(m * 8, 8)
        vals = [tx_ref[k, pl.ds(m8, 8), :] for k in range(3)] + [sl_ref[pl.ds(m8, 8), :]]
        for w in range(9):
            idx = tab_ref[T_FORC + w]
            for k in range(4):
                jf_ref[k, w, pl.ds(m8, 8), :] = take(vals[k], idx)

    pl.loop(3, NB + nch)(expand_forc)

    @pl.when(nch == 0)
    def _():
        for w in range(9):
            for k in range(4):
                jf_ref[k, w, MAIN : MAIN + 8, :] = jnp.full((8, 128), FAR if k < 3 else 0.0, f32)

    def forc_i(ic):
        i8 = pl.multiple_of(ic * 8, 8)
        xi, yi, zi, si = [spread(jf_ref[k, 4, pl.ds(i8, 8), :]) for k in range(4)]
        return jnp.where(xi > 0.5 * FAR, -FAR, xi), yi, zi, si

    def forc_j(acc, it, jc, count):
        for m in range(count):
            j8 = pl.multiple_of((jc + m) * 8, 8)
            for w in range(9):
                vals = [jf_ref[k, w, pl.ds(j8, 8), :] for k in range(4)]
                out = force_tile(*it, *vals, w == 4)
                acc = tuple(a + o for a, o in zip(acc, out))
        return acc

    def forc_store(acc, it, ic):
        i8 = pl.multiple_of(ic * 8, 8)
        keep = it[0] > -0.5 * FAR
        fback = tab_ref[T_FBACK]
        em = spread(take(em_ref[pl.ds(i8, 8), :], tab_ref[T_FORC + 4]))
        res = [total(a) for a in acc]
        res[3] = em + 0.5 * res[3]
        for k in range(4):
            tf_ref[k, pl.ds(i8, 8), :] = take(jnp.where(keep, res[k], 0.0), fback)

    zeros4 = (zero, zero, zero, zero)
    tf_ref[...] = jnp.zeros_like(tf_ref)

    def forc_main(n):
        ic = n + 6
        it = forc_i(ic)
        acc = forc_j(zeros4, it, n + 3, 7)
        acc = forc_j(acc, it, NB, 1)
        acc = lax.fori_loop(1, nch, lambda q, a: forc_j(a, it, NB + q, 1), acc)
        forc_store(acc, it, ic)

    pl.loop(0, 16)(forc_main)

    def forc_over(q):
        ic = NB + q
        it = forc_i(ic)
        acc = lax.fori_loop(0, 25, lambda g, a: forc_j(a, it, 3 + g, 1), zeros4)
        acc = lax.fori_loop(0, nch, lambda p, a: forc_j(a, it, NB + p, 1), acc)
        forc_store(acc, it, ic)

    pl.loop(0, nch)(forc_over)

    row16 = lax.broadcasted_iota(jnp.int32, (16, 256), 0)
    oiota = lax.broadcasted_iota(jnp.int32, (256, 128), 0).astype(f32)

    def gather(half):
        trans = [tf_ref[k, 256 * half : 256 * half + 256, :].T[0:16] for k in range(4)]
        parts = [p for v in trans for p in split3(v)]
        acc = None
        for c in range(16):
            col = (c // 4 + 2) * 8 + c % 4 + 2
            lhs = jnp.concatenate([jnp.where(row16 == c, p, 0.0) for p in parts], axis=0)
            drow = dest_ref[col : col + 1, 64:192] - float(256 * half)
            oh = jnp.where(oiota == drow, 1.0, 0.0)
            out = jnp.dot(lhs, oh, preferred_element_type=f32)
            acc = out if acc is None else acc + out
        return [acc[48 * k : 48 * k + 16] + acc[48 * k + 16 : 48 * k + 32] + acc[48 * k + 32 : 48 * k + 48] for k in range(4)]

    res = gather(0)
    for k in range(3):
        force_ref[k] = res[k]
    energy_ref[...] = res[3]

    @pl.when(nch > 4)
    def _():
        more = gather(1)
        for k in range(3):
            force_ref[k] = force_ref[k] + more[k]
        energy_ref[...] = energy_ref[...] + more[3]


def local(halo):
    upper = jnp.asarray(np.triu(np.ones((256, 256), np.float32), 1))
    tabs = jnp.asarray(index_tables())
    vm = pl.BlockSpec(memory_space=pltpu.VMEM)
    f32 = jnp.float32
    return pl.pallas_call(
        kernel,
        out_shape=(jax.ShapeDtypeStruct((3, 16, 128), f32), jax.ShapeDtypeStruct((16, 128), f32)),
        in_specs=[vm, vm, vm],
        out_specs=(vm, vm),
        scratch_shapes=[
            pltpu.VMEM((64, 256), f32),
            pltpu.VMEM((3, 128, NSLOT), f32),
            pltpu.VMEM((3, NSLOT, 128), f32),
            pltpu.VMEM((NSLOT, 128), f32),
            pltpu.VMEM((NSLOT, 128), f32),
            pltpu.VMEM((NSLOT, 128), f32),
            pltpu.VMEM((3, 21, NSLOT, 128), f32),
            pltpu.VMEM((4, 9, NSLOT, 128), f32),
            pltpu.VMEM((4, NSLOT, 128), f32),
        ],
        compiler_params=pltpu.CompilerParams(vmem_limit_bytes=60 * 1024 * 1024),
    )(halo, upper, tabs)


def with_halo(value, sides):
    for axis, dim, width in sides:
        count, length = (lax.axis_size(axis), value.shape[dim])
        up = [(i, (i + 1) % count) for i in range(count)]
        down = [(j, i) for i, j in up]
        last = lax.slice_in_dim(value, length - width, length, axis=dim)
        first = lax.slice_in_dim(value, 0, width, axis=dim)
        before = lax.ppermute(last, axis, up)
        after = lax.ppermute(first, axis, down)
        value = jnp.concatenate([before, value, after], axis=dim)
    return value


def on_device(positions, counts):
    cx, cy, cz = counts.shape
    slot = lax.broadcasted_iota(jnp.int32, (cx, cy, cz, SLOTS), 3)
    occupied = (slot < counts[..., None]).reshape(1, cx, cy, cz * SLOTS)
    packed = jnp.where(occupied, positions, 1.0e6)
    halo = with_halo(packed, (("gz", 3, SLOTS), ("gx", 1, 2), ("gy", 2, 2)))
    forces, energy = local(halo.reshape(3, 64, 256))
    return forces.reshape(3, cx, cy, cz * SLOTS), energy.reshape(cx, cy, cz * SLOTS)


def solution(mesh):
    return jax.shard_map(
        on_device,
        mesh=mesh,
        in_specs=(P(None, "gx", "gy", "gz"), P("gx", "gy", "gz")),
        out_specs=(P(None, "gx", "gy", "gz"), P("gx", "gy", "gz")),
        check_vma=False,
    )
```

time: 245 us -> 101 us (0.41)
  other arithmetic: 179 us -> 1.01 us
  Pallas kernels: 0 us -> 61.7 us
  starting transfers between devices: 45.5 us -> 29.4 us
  local copies, waits for them, and re-layouts: 8.04 us -> 1.72 us
  waiting for transfers between devices: 11 us -> 6.48 us
    reduce_sum x22 -> x0, other arithmetic: 176 us -> none  [the longest x13 135 us: cell_forces(): jnp.sum(factor * displace[component], axis=-1)]
    pallas_call x0 -> x1, Pallas kernels: none -> 61.7 us  [local(): pl.pallas_call(kernel, out_shape=(jax.ShapeDtypeStruct((3, 16, 128), f32)...]
    ppermute x6 -> x3, starting transfers between devices: 35.4 us -> 23.4 us  [with_halo(): after = lax.ppermute(first, axis, down)]
    reduce_sum x60 -> x0, local copies, waits for them, and re-layouts: 5.18 us -> none  [the longest x30 2.59 us: cell_forces(): jnp.sum(factor * displace[component], axis=-1)]
    ppermute x6 -> x3, starting transfers between devices: 10.1 us -> 5.96 us  [with_halo(): before = lax.ppermute(last, axis, up)]
    ppermute x6 -> x3, waiting for transfers between devices: 8.04 us -> 4.85 us  [with_halo(): after = lax.ppermute(first, axis, down)]
  transfers between devices with their start and end apart: 12 -> 6, of which waited for: 6 -> 4; matrix products, arithmetic and copies ran while one was open for 0% -> 0% of each run, Pallas kernels for 0% -> 0%
where the time goes in v1:
time: 101 us
  Pallas kernels  61.7 us (61%)
  starting transfers between devices  29.4 us (29%)
  waiting for transfers between devices  6.48 us (6%)
  local copies, waits for them, and re-layouts  1.72 us (2%)
  other arithmetic  1.01 us (1%)
    pallas_call x1, Pallas kernels, local(): pl.pallas_call(kernel, out_shape=(jax.ShapeDtypeStruct((3, 16, 128), f32)...  61.7 us
    ppermute x3, starting transfers between devices, with_halo(): after = lax.ppermute(first, axis, down)  23.4 us
    ppermute x3, starting transfers between devices, with_halo(): before = lax.ppermute(last, axis, up)  5.96 us
    ppermute x3, waiting for transfers between devices, with_halo(): after = lax.ppermute(first, axis, down)  4.85 us
  transfers between devices with their start and end apart: 6, of which 4 were waited for; matrix products, arithmetic and copies ran while one was open for 0% of the time, Pallas kernels for 0%

profile of v1, /device:TPU:24, one launch (start us, length us, event | category | flops | bytes accessed | tf_op | source)
XLA Modules:
  0.0 101.0 jit_solution(7151260114584290813)
XLA Ops:
  0.6 0.1 iota.12
  0.7 0.8 copy.6
  1.5 0.0 copy-start
  1.5 0.1 lt.14
  1.6 0.1 lt.15
  1.7 0.6 copy-done
  2.3 0.1 fusion.2
  2.3 0.0 collective-permute-start
  2.3 3.0 %collective-permute-start.1 = (f32[3,4,4,64]{3,2,1,0:T(4,128)S(1)}, f32[3,4,4,64]{3,2,1,0:T(4,128)S(1)}, u32[]{:S(2)}, u32[]{:S(2)}) collective-permute-start(f32[3,4,4,64]{3,2,1,0:T(4,128)S(1)} %get-tuple-element.11), channel_id=1, source_target_pairs={{1,0},{2,1},{3,2},{4,3},{5,4},{6,5},{7,6},{0,7},{9,8},{10,9},{11,1... | collective-permute-start | bytes 36872 | tf_op jit(solution)/shard_map/ppermute | solution.py:422
  5.3 1.5 %collective-permute-done = f32[3,4,4,64]{3,2,1,0:T(4,128)S(1)} collective-permute-done((f32[3,4,4,64]{3,2,1,0:T(4,128)S(1)}, f32[3,4,4,64]{3,2,1,0:T(4,128)S(1)}, u32[]{:S(2)}, u32[]{:S(2)}) %collective-permute-start) | collective-permute-done | bytes 12320 | tf_op jit(solution)/shard_map/ppermute | solution.py:421
  6.8 0.0 collective-permute-done.1
  6.8 0.1 pad_maximum_fusion.1
  6.9 3.8 %collective-permute-start.2 = (f32[3,2,4,256]{3,2,1,0:T(4,128)S(1)}, f32[3,2,4,256]{3,2,1,0:T(4,128)S(1)}, u32[]{:S(2)}, u32[]{:S(2)}) collective-permute-start(f32[3,2,4,256]{3,2,1,0:T(4,128)S(1)} %get-tuple-element.8), channel_id=1, source_target_pairs={{0,32},{32,64},{64,96},{96,128},{128,160},{160,192},{192,224},{224... | collective-permute-start | bytes 73736 | tf_op jit(solution)/shard_map/ppermute | solution.py:421
  10.8 16.8 %collective-permute-start.3 = (f32[3,2,4,256]{3,2,1,0:T(4,128)S(1)}, f32[3,2,4,256]{3,2,1,0:T(4,128)S(1)}, u32[]{:S(2)}, u32[]{:S(2)}) collective-permute-start(f32[3,2,4,256]{3,2,1,0:T(4,128)S(1)} %get-tuple-element.9), channel_id=1, source_target_pairs={{32,0},{64,32},{96,64},{128,96},{160,128},{192,160},{224,192},{256... | collective-permute-start | bytes 73736 | tf_op jit(solution)/shard_map/ppermute | solution.py:422
  27.6 0.0 collective-permute-done.2
  27.6 1.5 %collective-permute-done.3 = f32[3,2,4,256]{3,2,1,0:T(4,128)S(1)} collective-permute-done((f32[3,2,4,256]{3,2,1,0:T(4,128)S(1)}, f32[3,2,4,256]{3,2,1,0:T(4,128)S(1)}, u32[]{:S(2)}, u32[]{:S(2)}) %collective-permute-start.3) | collective-permute-done | bytes 24608 | tf_op jit(solution)/shard_map/ppermute | solution.py:422
  29.1 0.1 pad_maximum_fusion
  29.2 2.1 %collective-permute-start.4 = (f32[3,8,2,256]{3,2,1,0:T(2,128)S(1)}, f32[3,8,2,256]{3,2,1,0:T(2,128)S(1)}, u32[]{:S(2)}, u32[]{:S(2)}) collective-permute-start(f32[3,8,2,256]{3,2,1,0:T(2,128)S(1)} %get-tuple-element.6), channel_id=1, source_target_pairs={{0,8},{8,16},{16,24},{24,0},{1,9},{9,17},{17,25},{25,1},{2,10},{10... | collective-permute-start | bytes 147464 | tf_op jit(solution)/shard_map/ppermute | solution.py:421
  31.4 3.7 %collective-permute-start.5 = (f32[3,8,2,256]{3,2,1,0:T(2,128)S(1)}, f32[3,8,2,256]{3,2,1,0:T(2,128)S(1)}, u32[]{:S(2)}, u32[]{:S(2)}) collective-permute-start(f32[3,8,2,256]{3,2,1,0:T(2,128)S(1)} %get-tuple-element.7), channel_id=1, source_target_pairs={{8,0},{16,8},{24,16},{0,24},{9,1},{17,9},{25,17},{1,25},{10,2},{18... | collective-permute-start | bytes 147464 | tf_op jit(solution)/shard_map/ppermute | solution.py:422
  35.1 0.1 collective-permute-done.4
  35.2 3.3 %collective-permute-done.5 = f32[3,8,2,256]{3,2,1,0:T(2,128)S(1)} collective-permute-done((f32[3,8,2,256]{3,2,1,0:T(2,128)S(1)}, f32[3,8,2,256]{3,2,1,0:T(2,128)S(1)}, u32[]{:S(2)}, u32[]{:S(2)}) %collective-permute-start.5) | collective-permute-done | bytes 49184 | tf_op jit(solution)/shard_map/ppermute | solution.py:422
  38.6 0.8 maximum_bitcast_fusion.h_ref
  39.3 61.7 %shard_map.59 = (f32[3,16,128]{2,1,0:T(8,128)}, f32[16,128]{1,0:T(8,128)}) custom-call(f32[3,64,256]{2,1,0:T(8,128)} %maximum_bitcast_fusion.h_ref, f32[256,256]{1,0:T(8,128)} %constant.6.clone.u_ref, s32[37,8,128]{2,1,0:T(8,128)} %constant.7.clone.tab_ref), custom_call_target="tpu_custom_call" | custom-call | tf_op jit(solution)/shard_map/pallas_call | solution.py:394
  (5 shorter events, 0.1 us)
Async XLA Ops:
  1.5 0.7 copy-start
  2.3 4.5 %collective-permute-start = (f32[3,4,4,64]{3,2,1,0:T(4,128)S(1)}, f32[3,4,4,64]{3,2,1,0:T(4,128)S(1)}, u32[]{:S(2)}, u32[]{:S(2)}) collective-permute-start(f32[3,4,4,64]{3,2,1,0:T(4,128)S(1)} %get-tuple-element.10), channel_id=1, source_target_pairs={{0,1},{1,2},{2,3},{3,4},{4,5},{5,6},{6,7},{7,0},{8,9},{9,10},{10,1... | collective-permute-start | bytes 36872 | tf_op jit(solution)/shard_map/ppermute | solution.py:421
  2.3 4.5 %collective-permute-start.1 = (f32[3,4,4,64]{3,2,1,0:T(4,128)S(1)}, f32[3,4,4,64]{3,2,1,0:T(4,128)S(1)}, u32[]{:S(2)}, u32[]{:S(2)}) collective-permute-start(f32[3,4,4,64]{3,2,1,0:T(4,128)S(1)} %get-tuple-element.11), channel_id=1, source_target_pairs={{1,0},{2,1},{3,2},{4,3},{5,4},{6,5},{7,6},{0,7},{9,8},{10,9},{11,1... | collective-permute-start | bytes 36872 | tf_op jit(solution)/shard_map/ppermute | solution.py:422
  6.9 20.6 %collective-permute-start.2 = (f32[3,2,4,256]{3,2,1,0:T(4,128)S(1)}, f32[3,2,4,256]{3,2,1,0:T(4,128)S(1)}, u32[]{:S(2)}, u32[]{:S(2)}) collective-permute-start(f32[3,2,4,256]{3,2,1,0:T(4,128)S(1)} %get-tuple-element.8), channel_id=1, source_target_pairs={{0,32},{32,64},{64,96},{96,128},{128,160},{160,192},{192,224},{224... | collective-permute-start | bytes 73736 | tf_op jit(solution)/shard_map/ppermute | solution.py:421
  10.8 18.3 %collective-permute-start.3 = (f32[3,2,4,256]{3,2,1,0:T(4,128)S(1)}, f32[3,2,4,256]{3,2,1,0:T(4,128)S(1)}, u32[]{:S(2)}, u32[]{:S(2)}) collective-permute-start(f32[3,2,4,256]{3,2,1,0:T(4,128)S(1)} %get-tuple-element.9), channel_id=1, source_target_pairs={{32,0},{64,32},{96,64},{128,96},{160,128},{192,160},{224,192},{256... | collective-permute-start | bytes 73736 | tf_op jit(solution)/shard_map/ppermute | solution.py:422
  29.2 6.0 %collective-permute-start.4 = (f32[3,8,2,256]{3,2,1,0:T(2,128)S(1)}, f32[3,8,2,256]{3,2,1,0:T(2,128)S(1)}, u32[]{:S(2)}, u32[]{:S(2)}) collective-permute-start(f32[3,8,2,256]{3,2,1,0:T(2,128)S(1)} %get-tuple-element.6), channel_id=1, source_target_pairs={{0,8},{8,16},{16,24},{24,0},{1,9},{9,17},{17,25},{25,1},{2,10},{10... | collective-permute-start | bytes 147464 | tf_op jit(solution)/shard_map/ppermute | solution.py:421
  31.4 7.2 %collective-permute-start.5 = (f32[3,8,2,256]{3,2,1,0:T(2,128)S(1)}, f32[3,8,2,256]{3,2,1,0:T(2,128)S(1)}, u32[]{:S(2)}, u32[]{:S(2)}) collective-permute-start(f32[3,8,2,256]{3,2,1,0:T(2,128)S(1)} %get-tuple-element.7), channel_id=1, source_target_pairs={{8,0},{16,8},{24,16},{0,24},{9,1},{17,9},{25,17},{1,25},{10,2},{18... | collective-permute-start | bytes 147464 | tf_op jit(solution)/shard_map/ppermute | solution.py:422

commit v2 on v1

v2 whole, which is shorter than its diff:
```python
import functools

import jax
import jax.numpy as jnp
import numpy as np
from jax import lax
from jax.experimental import pallas as pl
from jax.experimental.pallas import tpu as pltpu
from jax.sharding import PartitionSpec as P

SLOTS = 64
lattice_const = 3.615
SPAN_XY = 2.0 * lattice_const
SPAN_Z = 4.0 * lattice_const
cut_radius = 5.50679
cut_width = 0.50037
dens_scale = 3.80362
beta_one = 0.17394
radius_three = -2.19885
energy_one = 201.458
energy_two = 0.00659288
radius_one = 0.83591
radius_two = 4.46867
alpha_one = 2.97758
alpha_two = 1.54927
shift_delta = 0.0086225
repulsion = ((4.0, 2.24), (40.0, 1.8), (1150.0, 1.2))
embed_zero = -2.28235
embed_curve = 1.35535
lower_terms = (-1.27775, -0.86074, 1.78804, 2.97571)
upper_quartic = 0.4
upper_damping = 0.3
LOG2E = 1.4426950408889634

HB = 1.836
ZOFF = 0.228
NB = 28
CAP = 8
MAIN = NB * CAP
NSLOT = 512
NCHUNK = NSLOT // 8
FAR = 1000.0


def index_tables():
    lane = np.arange(128)
    sub = np.arange(8)[:, None]
    unit = lane // 8
    cols = [unit, 16 + unit, 32 + unit % 4]
    rows = []
    for ce in cols:
        for dx in (-1, 0, 1):
            for dy in (-1, 0, 1):
                rows.append((ce // 6 + 1 + dx) * 8 + ce % 6 + 1 + dy)
    for dx in (-1, 0, 1):
        for dy in (-1, 0, 1):
            rows.append((unit // 4 + 2 + dx) * 8 + unit % 4 + 2 + dy)
    rows = np.stack(rows + [rows[0]] * 4).astype(np.int32)
    back, mask = [], []
    x, y = lane // 8 - 1, lane % 8 - 1
    inside = (lane < 64) & (x >= 0) & (x < 6) & (y >= 0) & (y < 6)
    ce = np.where(inside, x * 6 + y, 0)
    for t, (lo, hi) in enumerate(((0, 16), (16, 32), (32, 36))):
        ok = inside & (ce >= lo) & (ce < hi)
        back.append(np.where(ok, (ce - lo) * 8, 0) + sub)
        mask.append(np.broadcast_to(ok.astype(np.int32), (8, 128)))
    fback = np.where(lane < 16, lane * 8, 0) + sub
    return rows, np.stack(back + mask + [fback]).astype(np.int32)


W_FORC, W_ALL = 27, 36
T_BACK, T_MASK, T_FBACK = 0, 3, 6
SIGMA = float(np.sqrt(beta_one * LOG2E))
TAPER_K = float((SIGMA * cut_width) ** 4)
LN2 = float(np.log(2.0))


def split3(v):
    hi = v.astype(jnp.bfloat16).astype(jnp.float32)
    rest = v - hi
    mid = rest.astype(jnp.bfloat16).astype(jnp.float32)
    return hi, mid, rest - mid


def embedding(density):
    e = density - 1.0
    e2 = e * e
    e3 = e2 * e
    l0, l1, l2, l3 = lower_terms
    low = embed_zero + e2 * (0.5 * embed_curve + e * (l0 + e * (l1 + e * (l2 + e * l3))))
    lows = e * (embed_curve + e * (3.0 * l0 + e * (4.0 * l1 + e * (5.0 * l2 + e * (6.0 * l3)))))
    num = embed_zero + e2 * (0.5 * embed_curve + e * (l0 + e * upper_quartic))
    nums = e * (embed_curve + e * (3.0 * l0 + e * (4.0 * upper_quartic)))
    below = e < 0.0
    den = jnp.where(below, 1.0, 1.0 + upper_damping * e3)
    inv = 1.0 / den
    up = num * inv
    ups = (nums * den - num * (3.0 * upper_damping) * e2) * inv * inv
    return jnp.where(below, low, up), jnp.where(below, lows, ups)


def geometry(xi, yi, zi, xj, yj, zj, mask_self):
    dx, dy, dz = xj - xi, yj - yi, zj - zi
    r2 = dx * dx + dy * dy + dz * dz
    if mask_self:
        r2 = jnp.where(r2 < 0.25 * SIGMA**2, 25.0, r2)
    rinv = lax.rsqrt(r2)
    return dx, dy, dz, rinv, r2 * rinv


def taper_parts(r):
    t = jnp.minimum(r - cut_radius * SIGMA, 0.0)
    t2 = t * t
    q = t2 * t2
    root = lax.rsqrt(q + TAPER_K)
    return t, t2, q, root * root


def gaussian(r):
    rs = r - radius_three * SIGMA
    return rs, jnp.exp2(float(np.log2(dens_scale)) - rs * rs)


def rho_tile(xi, yi, zi, xj, yj, zj, mask_self):
    _, _, _, _, r = geometry(xi, yi, zi, xj, yj, zj, mask_self)
    _, _, q, inv = taper_parts(r)
    _, g = gaussian(r)
    return g * (q * inv)


def force_tile(xi, yi, zi, si, xj, yj, zj, sj, mask_self, terms):
    dx, dy, dz, rinv, r = geometry(xi, yi, zi, xj, yj, zj, mask_self)
    t, t2, q, inv = taper_parts(r)
    taper = q * inv
    tslope = (t * t2) * (inv * inv)
    rs, g = gaussian(r)
    dslope = g * (rs * taper * (-2.0 * LN2 / (4.0 * TAPER_K)) + tslope)
    k1, k2 = alpha_one / SIGMA, alpha_two / SIGMA
    u1 = jnp.exp2(r * (-k1 * LOG2E) + alpha_one * LOG2E * radius_one)
    u2 = jnp.exp2(r * (-k2 * LOG2E) + alpha_two * LOG2E * radius_two)
    y1 = u1 * (u1 - 1.0)
    y2 = u2 * (u2 - 1.0)
    base = (y1 - u1) * energy_one + ((y2 - u2) * energy_two + shift_delta)
    bslope = y1 * (-2.0 * k1 * energy_one / (4.0 * TAPER_K)) + y2 * (-2.0 * k2 * energy_two / (4.0 * TAPER_K))
    pval = base * taper
    pslope = bslope * taper + base * tslope
    rep = None
    for strength, reach in repulsion[:terms]:
        s = jnp.maximum(reach * SIGMA - r, 0.0)
        g3 = (s * s) * (s * (strength / (SIGMA**4 * TAPER_K)))
        pslope = pslope + g3
        rep = g3 * s if rep is None else rep + g3 * s
    f = (pslope + (si + sj) * dslope) * rinv
    return f * dx, f * dy, f * dz, pval, rep


def kernel(h_ref, row_ref, tab_ref, force_ref, energy_ref,
           dest_ref, tc_ref, tx_ref, rm_ref, rho_ref, sl_ref, em_ref, jd_ref, jf_ref, tf_ref):
    f32 = jnp.float32
    row = lax.broadcasted_iota(jnp.int32, (64, 256), 0)
    lane = lax.broadcasted_iota(jnp.int32, (64, 256), 1)
    za = h_ref[2] + (lane // 64 - 1).astype(f32) * SPAN_Z
    pos = [
        split3((h_ref[0] + (row // 8 - 2).astype(f32) * SPAN_XY) * SIGMA),
        split3((h_ref[1] + (row % 8 - 2).astype(f32) * SPAN_XY) * SIGMA),
        split3(za * SIGMA),
    ]
    fb = jnp.floor((za + (ZOFF + 6 * HB)) * (1.0 / HB))
    valid = (fb >= 0.0) & (fb < float(NB))
    bins = jnp.where(valid, fb, -1.0)

    irow = lax.broadcasted_iota(jnp.int32, (256, 256), 0)
    ilane = lax.broadcasted_iota(jnp.int32, (256, 256), 1)
    upper = jnp.where(irow < ilane, 1.0, 0.0)
    fold = jnp.where(irow[0:8] == ilane[0:8] // 32, 1.0, 0.0)
    biota = lax.broadcasted_iota(jnp.int32, (32, 256), 0).astype(f32)
    ranks = []
    for g in range(8):
        ob = jnp.concatenate(
            [jnp.where(bins[8 * g + u : 8 * g + u + 1, :] == biota, 1.0, 0.0) for u in range(8)], axis=0
        )
        pr = ob * jnp.dot(ob, upper, preferred_element_type=f32)
        ranks.append(jnp.dot(fold, pr, preferred_element_type=f32))
    rank = jnp.concatenate(ranks, axis=0)
    over = valid & (rank >= float(CAP))
    orank = jnp.dot(jnp.where(over, 1.0, 0.0), upper, preferred_element_type=f32)
    novf = jnp.max(jnp.where(over, orank + 1.0, 0.0)).astype(jnp.int32)
    nch = (novf + 7) // 8
    dest = jnp.where(over, orank + float(MAIN), bins * float(CAP) + rank)
    dest_ref[...] = jnp.where(valid, dest, -1.0)

    tc_ref[:, 192:256, :] = jnp.zeros((3, 64, NSLOT), f32)
    ones = jnp.where(valid, 1.0, 0.0)
    siota = irow.astype(f32)
    sub8 = lax.broadcasted_iota(jnp.int32, (8, 256), 0)

    def scatter(half):
        for g in range(8):
            parts = [p[8 * g : 8 * g + 8] for trio in pos for p in trio] + [ones[8 * g : 8 * g + 8]]
            acc = None
            for u in range(8):
                lhs = jnp.concatenate([jnp.where(sub8 == u, p, 0.0) for p in parts], axis=0)
                drow = dest_ref[8 * g + u : 8 * g + u + 1, :] - float(256 * half)
                oh = jnp.where(siota == drow, 1.0, 0.0)
                out = lax.dot_general(lhs, oh, (((1,), (1,)), ((), ())), preferred_element_type=f32)
                acc = out if acc is None else acc + out
            have = acc[72:80] > 0.5
            for k in range(3):
                for p in range(3):
                    v = acc[24 * k + 8 * p : 24 * k + 8 * p + 8]
                    if p == 0:
                        v = jnp.where(have, v, FAR)
                    tc_ref[k, 64 * p + 8 * g : 64 * p + 8 * g + 8, 256 * half : 256 * half + 256] = v

    def transpose(half):
        for k in range(3):
            tx_ref[k, 256 * half : 256 * half + 256, :] = tc_ref[k, :, 256 * half : 256 * half + 256].T

    scatter(0)
    transpose(0)

    @pl.when(nch > 4)
    def _():
        scatter(1)
        transpose(1)

    def take(values, idx):
        return jnp.take_along_axis(values, idx, axis=1, mode="promise_in_bounds")

    source = jnp.where(irow[:, 0:128] < 192, irow[:, 0:128] % 64, -1)

    def spreader(w):
        m = jnp.where(source == row_ref[w : w + 1, :], 1.0, 0.0)
        rm_ref[w] = m
        return m

    def expand(values, first, count, out_ref, stride, comps):
        for w in range(0, count, 2):
            pair = [spreader(first + v) if comps[0] == 0 else rm_ref[first + v] for v in (w, w + 1) if v < count]
            mat = jnp.concatenate(pair, axis=1) if len(pair) == 2 else pair[0]
            for k, vals in zip(comps, values):
                out = jnp.dot(vals, mat, preferred_element_type=f32)
                for v in range(len(pair)):
                    for m in range(NB + 1):
                        out_ref[w + v, m * stride + k] = out[8 * m : 8 * m + 8, 128 * v : 128 * v + 128]

    def expand_more(values, first, count, out_ref, stride, comps, nch):
        def chunk(q):
            m8 = pl.multiple_of((NB + q) * 8, 8)

            def one(w):
                mat = rm_ref[first + w]
                for k, ref in zip(comps, values):
                    out_ref[w, (NB + q) * stride + k] = jnp.dot(ref[pl.ds(m8, 8), :], mat, preferred_element_type=f32)

            pl.loop(0, count)(one)

        pl.loop(1, nch)(chunk)

    rows = (NB + 1) * 8
    txk = [tx_ref.at[k] for k in range(3)]
    expand([tx_ref[k, 0:rows, :] for k in range(3)], 0, 27, jd_ref, 3, (0, 1, 2))
    expand([tx_ref[k, 0:rows, :] for k in range(3)], W_FORC, 9, jf_ref, 4, (0, 1, 2))
    expand_more(txk, 0, 27, jd_ref, 3, (0, 1, 2), nch)
    expand_more(txk, W_FORC, 9, jf_ref, 4, (0, 1, 2), nch)

    sub = lax.broadcasted_iota(jnp.int32, (8, 128), 0)
    lane128 = lax.broadcasted_iota(jnp.int32, (8, 128), 1)
    diag = sub == lane128 % 8

    def spread(v):
        return jnp.broadcast_to(jnp.sum(jnp.where(diag, v, 0.0), axis=0, keepdims=True), (8, 128))

    def total(v):
        return jnp.broadcast_to(jnp.sum(v, axis=0, keepdims=True), (8, 128))

    rho_ref[...] = jnp.ones_like(rho_ref)
    zero = jnp.zeros((8, 128), f32)

    def dens_i(t, ic):
        xi, yi, zi = [spread(jd_ref[9 * t + 4, ic * 3 + k]) for k in range(3)]
        return jnp.where(xi > 0.5 * FAR, -FAR, xi), yi, zi

    def dens_j(acc, it, t, jc, count):
        for m in range(count):
            for s in range(9):
                xj, yj, zj = [jd_ref[9 * t + s, (jc + m) * 3 + k] for k in range(3)]
                acc = acc + rho_tile(*it, xj, yj, zj, s == 4)
        return acc

    def dens_rest(acc, it, t):
        acc = dens_j(acc, it, t, NB, 1)
        return lax.fori_loop(1, nch, lambda q, a: dens_j(a, it, t, NB + q, 1), acc)

    def dens_store(acc, t, ic, group=0):
        i8 = pl.multiple_of(ic * 8, 8)
        got = take(acc, tab_ref[T_BACK + t] + 32 * group)
        rho_ref[pl.ds(i8, 8), :] = jnp.where(tab_ref[T_MASK + t] > 0, got, rho_ref[pl.ds(i8, 8), :])

    def dens_main(n):
        e, t = n // 2, n % 2
        it = dens_i(t, e + 3)
        acc = dens_rest(dens_j(zero, it, t, e, 7), it, t)
        dens_store(total(acc), t, e + 3)

    pl.loop(0, 44)(dens_main)

    def dens_corner(n):
        e = jnp.minimum(4 * n, 18)
        its = [dens_i(2, e + 3 + u) for u in range(4)]
        it = its[0]
        for u in range(1, 4):
            it = tuple(jnp.where(lane128 // 32 == u, b, a) for a, b in zip(it, its[u]))
        acc = total(dens_rest(dens_j(zero, it, 2, e, 10), it, 2))
        for u in range(4):
            dens_store(acc, 2, e + 3 + u, u)

    pl.loop(0, 6)(dens_corner)

    def dens_over(n):
        q, t = n // 3, n % 3
        ic = NB + q
        it = dens_i(t, ic)
        acc = lax.fori_loop(0, 4, lambda g, a: dens_j(a, it, t, 7 * g, 7), zero)
        acc = lax.fori_loop(0, nch, lambda p, a: dens_j(a, it, t, NB + p, 1), acc)
        dens_store(total(acc), t, ic)

    pl.loop(0, 3 * nch)(dens_over)

    low = lax.broadcasted_iota(jnp.int32, (256, 128), 1) < 64

    def embed_rows(start):
        occ = tx_ref[0, start : start + 256, 0:128] < 0.5 * FAR
        val, slo = embedding(rho_ref[start : start + 256, :])
        em_ref[start : start + 256, :] = jnp.where(occ, val, 0.0)
        hi, mid, lo = split3(jnp.where(occ & low, slo, 0.0))
        sl_ref[start : start + 256, 0:128] = hi + pltpu.roll(mid, 64, 1)
        sl_ref[start : start + 256, 128:256] = lo

    embed_rows(0)

    @pl.when(nch > 4)
    def _():
        embed_rows(256)

    expand([sl_ref[0:rows, :]], W_FORC, 9, jf_ref, 4, (3,))
    expand_more([sl_ref], W_FORC, 9, jf_ref, 4, (3,), nch)

    def forc_i(ic):
        xi, yi, zi, si = [spread(jf_ref[4, ic * 4 + k]) for k in range(4)]
        return jnp.where(xi > 0.5 * FAR, -FAR, xi), yi, zi, si

    def forc_j(acc, it, jc, terms):
        for m, n in enumerate(terms):
            for s in range(9):
                vals = [jf_ref[s, (jc + m) * 4 + k] for k in range(4)]
                out = force_tile(*it, *vals, s == 4, n)
                acc = tuple(a if o is None else a + o for a, o in zip(acc, out))
        return acc

    def forc_store(acc, it, ic):
        i8 = pl.multiple_of(ic * 8, 8)
        keep = it[0] > -0.5 * FAR
        idx = jnp.broadcast_to(row_ref[W_FORC + 4 : W_FORC + 5, :], (8, 128))
        em = spread(take(em_ref[pl.ds(i8, 8), :], idx))
        res = [total(a) * (SIGMA * 4.0 * TAPER_K) for a in acc[:3]]
        res.append(em + 0.5 * total(acc[3] - TAPER_K * acc[4]))
        for k in range(4):
            tf_ref[k, pl.ds(i8, 8), :] = take(jnp.where(keep, res[k], 0.0), tab_ref[T_FBACK])

    zeros5 = (zero,) * 5
    tf_ref[...] = jnp.zeros_like(tf_ref)

    def forc_main(n):
        ic = n + 6
        it = forc_i(ic)
        acc = forc_j(zeros5, it, n + 3, (0, 1, 3, 3, 3, 1, 0))
        acc = forc_j(acc, it, NB, (3,))
        acc = lax.fori_loop(1, nch, lambda q, a: forc_j(a, it, NB + q, (3,)), acc)
        forc_store(acc, it, ic)

    pl.loop(0, 16)(forc_main)

    def forc_over(q):
        ic = NB + q
        it = forc_i(ic)
        acc = lax.fori_loop(0, 5, lambda g, a: forc_j(a, it, 3 + 5 * g, (3,) * 5), zeros5)
        acc = lax.fori_loop(0, nch, lambda p, a: forc_j(a, it, NB + p, (3,)), acc)
        forc_store(acc, it, ic)

    pl.loop(0, nch)(forc_over)

    row16 = lax.broadcasted_iota(jnp.int32, (16, 256), 0)
    oiota = lax.broadcasted_iota(jnp.int32, (256, 128), 0).astype(f32)

    def gather(half):
        trans = [tf_ref[k, 256 * half : 256 * half + 256, :].T[0:16] for k in range(4)]
        parts = [p for v in trans for p in split3(v)]
        acc = None
        for c in range(16):
            col = (c // 4 + 2) * 8 + c % 4 + 2
            lhs = jnp.concatenate([jnp.where(row16 == c, p, 0.0) for p in parts], axis=0)
            drow = dest_ref[col : col + 1, 64:192] - float(256 * half)
            oh = jnp.where(oiota == drow, 1.0, 0.0)
            out = jnp.dot(lhs, oh, preferred_element_type=f32)
            acc = out if acc is None else acc + out
        return [acc[48 * k : 48 * k + 16] + acc[48 * k + 16 : 48 * k + 32] + acc[48 * k + 32 : 48 * k + 48] for k in range(4)]

    res = gather(0)
    for k in range(3):
        force_ref[k] = res[k]
    energy_ref[...] = res[3]

    @pl.when(nch > 4)
    def _():
        more = gather(1)
        for k in range(3):
            force_ref[k] = force_ref[k] + more[k]
        energy_ref[...] = energy_ref[...] + more[3]


def local(halo):
    rows, tabs = index_tables()
    vm = pl.BlockSpec(memory_space=pltpu.VMEM)
    f32 = jnp.float32
    return pl.pallas_call(
        kernel,
        out_shape=(jax.ShapeDtypeStruct((3, 16, 128), f32), jax.ShapeDtypeStruct((16, 128), f32)),
        in_specs=[vm, vm, vm],
        out_specs=(vm, vm),
        scratch_shapes=[
            pltpu.VMEM((64, 256), f32),
            pltpu.VMEM((3, 256, NSLOT), f32),
            pltpu.VMEM((3, NSLOT, 256), f32),
            pltpu.VMEM((W_ALL, 256, 128), f32),
            pltpu.VMEM((NSLOT, 128), f32),
            pltpu.VMEM((NSLOT, 256), f32),
            pltpu.VMEM((NSLOT, 128), f32),
            pltpu.VMEM((27, NCHUNK * 3, 8, 128), f32),
            pltpu.VMEM((9, NCHUNK * 4, 8, 128), f32),
            pltpu.VMEM((4, NSLOT, 128), f32),
        ],
        compiler_params=pltpu.CompilerParams(vmem_limit_bytes=60 * 1024 * 1024),
    )(halo, jnp.asarray(rows), jnp.asarray(tabs))


def with_halo(value, sides):
    for axis, dim, width in sides:
        count, length = (lax.axis_size(axis), value.shape[dim])
        up = [(i, (i + 1) % count) for i in range(count)]
        down = [(j, i) for i, j in up]
        last = lax.slice_in_dim(value, length - width, length, axis=dim)
        first = lax.slice_in_dim(value, 0, width, axis=dim)
        before = lax.ppermute(last, axis, up)
        after = lax.ppermute(first, axis, down)
        value = jnp.concatenate([before, value, after], axis=dim)
    return value


def on_device(positions, counts):
    cx, cy, cz = counts.shape
    slot = lax.broadcasted_iota(jnp.int32, (cx, cy, cz, SLOTS), 3)
    occupied = (slot < counts[..., None]).reshape(1, cx, cy, cz * SLOTS)
    packed = jnp.where(occupied, positions, 1.0e6)
    halo = with_halo(packed, (("gz", 3, SLOTS), ("gx", 1, 2), ("gy", 2, 2)))
    forces, energy = local(halo.reshape(3, 64, 256))
    return forces.reshape(3, cx, cy, cz * SLOTS), energy.reshape(cx, cy, cz * SLOTS)


def solution(mesh):
    return jax.shard_map(
        on_device,
        mesh=mesh,
        in_specs=(P(None, "gx", "gy", "gz"), P("gx", "gy", "gz")),
        out_specs=(P(None, "gx", "gy", "gz"), P("gx", "gy", "gz")),
        check_vma=False,
    )
```

time: 101 us -> 87.5 us (0.87)
  Pallas kernels: 61.7 us -> 47.7 us
    pallas_call x1, Pallas kernels: 61.7 us -> 47.7 us  [local(): pl.pallas_call(kernel, out_shape=(jax.ShapeDtypeStruct((3, 16, 128), f32)...]
where the time goes in v2:
time: 87.5 us; the launch traced here: 87 us
  Pallas kernels  47.7 us (55%)
  starting transfers between devices  29.4 us (34%)
  waiting for transfers between devices  6.48 us (7%)
  local copies, waits for them, and re-layouts  1.72 us (2%)
  other arithmetic  1.01 us (1%)
    pallas_call x1, Pallas kernels, local(): pl.pallas_call(kernel, out_shape=(jax.ShapeDtypeStruct((3, 16, 128), f32)...  47.7 us
    ppermute x3, starting transfers between devices, with_halo(): after = lax.ppermute(first, axis, down)  23.4 us
    ppermute x3, starting transfers between devices, with_halo(): before = lax.ppermute(last, axis, up)  5.96 us
    ppermute x3, waiting for transfers between devices, with_halo(): after = lax.ppermute(first, axis, down)  4.85 us
  transfers between devices with their start and end apart: 6, of which 4 were waited for; matrix products, arithmetic and copies ran while one was open for 0% of the time, Pallas kernels for 0%

profile of v2, /device:TPU:24, one launch (start us, length us, event | category | flops | bytes accessed | tf_op | source)
XLA Modules:
  0.0 87.0 jit_solution(7288874506408276367)
XLA Ops:
  0.6 0.1 iota.12
  0.7 0.8 copy.6
  1.5 0.0 copy-start
  1.5 0.1 lt.14
  1.6 0.1 lt.15
  1.7 0.6 copy-done
  2.3 0.1 fusion.2
  2.3 0.0 collective-permute-start
  2.3 3.0 %collective-permute-start.1 = (f32[3,4,4,64]{3,2,1,0:T(4,128)S(1)}, f32[3,4,4,64]{3,2,1,0:T(4,128)S(1)}, u32[]{:S(2)}, u32[]{:S(2)}) collective-permute-start(f32[3,4,4,64]{3,2,1,0:T(4,128)S(1)} %get-tuple-element.11), channel_id=1, source_target_pairs={{1,0},{2,1},{3,2},{4,3},{5,4},{6,5},{7,6},{0,7},{9,8},{10,9},{11,1... | collective-permute-start | bytes 36872 | tf_op jit(solution)/shard_map/ppermute | solution.py:455
  5.3 1.5 %collective-permute-done = f32[3,4,4,64]{3,2,1,0:T(4,128)S(1)} collective-permute-done((f32[3,4,4,64]{3,2,1,0:T(4,128)S(1)}, f32[3,4,4,64]{3,2,1,0:T(4,128)S(1)}, u32[]{:S(2)}, u32[]{:S(2)}) %collective-permute-start) | collective-permute-done | bytes 12320 | tf_op jit(solution)/shard_map/ppermute | solution.py:454
  6.8 0.0 collective-permute-done.1
  6.8 0.1 pad_maximum_fusion.1
  6.9 3.8 %collective-permute-start.2 = (f32[3,2,4,256]{3,2,1,0:T(4,128)S(1)}, f32[3,2,4,256]{3,2,1,0:T(4,128)S(1)}, u32[]{:S(2)}, u32[]{:S(2)}) collective-permute-start(f32[3,2,4,256]{3,2,1,0:T(4,128)S(1)} %get-tuple-element.8), channel_id=1, source_target_pairs={{0,32},{32,64},{64,96},{96,128},{128,160},{160,192},{192,224},{224... | collective-permute-start | bytes 73736 | tf_op jit(solution)/shard_map/ppermute | solution.py:454
  10.8 16.8 %collective-permute-start.3 = (f32[3,2,4,256]{3,2,1,0:T(4,128)S(1)}, f32[3,2,4,256]{3,2,1,0:T(4,128)S(1)}, u32[]{:S(2)}, u32[]{:S(2)}) collective-permute-start(f32[3,2,4,256]{3,2,1,0:T(4,128)S(1)} %get-tuple-element.9), channel_id=1, source_target_pairs={{32,0},{64,32},{96,64},{128,96},{160,128},{192,160},{224,192},{256... | collective-permute-start | bytes 73736 | tf_op jit(solution)/shard_map/ppermute | solution.py:455
  27.6 0.0 collective-permute-done.2
  27.6 1.5 %collective-permute-done.3 = f32[3,2,4,256]{3,2,1,0:T(4,128)S(1)} collective-permute-done((f32[3,2,4,256]{3,2,1,0:T(4,128)S(1)}, f32[3,2,4,256]{3,2,1,0:T(4,128)S(1)}, u32[]{:S(2)}, u32[]{:S(2)}) %collective-permute-start.3) | collective-permute-done | bytes 24608 | tf_op jit(solution)/shard_map/ppermute | solution.py:455
  29.1 0.1 pad_maximum_fusion
  29.2 2.1 %collective-permute-start.4 = (f32[3,8,2,256]{3,2,1,0:T(2,128)S(1)}, f32[3,8,2,256]{3,2,1,0:T(2,128)S(1)}, u32[]{:S(2)}, u32[]{:S(2)}) collective-permute-start(f32[3,8,2,256]{3,2,1,0:T(2,128)S(1)} %get-tuple-element.6), channel_id=1, source_target_pairs={{0,8},{8,16},{16,24},{24,0},{1,9},{9,17},{17,25},{25,1},{2,10},{10... | collective-permute-start | bytes 147464 | tf_op jit(solution)/shard_map/ppermute | solution.py:454
  31.4 3.7 %collective-permute-start.5 = (f32[3,8,2,256]{3,2,1,0:T(2,128)S(1)}, f32[3,8,2,256]{3,2,1,0:T(2,128)S(1)}, u32[]{:S(2)}, u32[]{:S(2)}) collective-permute-start(f32[3,8,2,256]{3,2,1,0:T(2,128)S(1)} %get-tuple-element.7), channel_id=1, source_target_pairs={{8,0},{16,8},{24,16},{0,24},{9,1},{17,9},{25,17},{1,25},{10,2},{18... | collective-permute-start | bytes 147464 | tf_op jit(solution)/shard_map/ppermute | solution.py:455
  35.1 0.1 collective-permute-done.4
  35.2 3.3 %collective-permute-done.5 = f32[3,8,2,256]{3,2,1,0:T(2,128)S(1)} collective-permute-done((f32[3,8,2,256]{3,2,1,0:T(2,128)S(1)}, f32[3,8,2,256]{3,2,1,0:T(2,128)S(1)}, u32[]{:S(2)}, u32[]{:S(2)}) %collective-permute-start.5) | collective-permute-done | bytes 49184 | tf_op jit(solution)/shard_map/ppermute | solution.py:455
  38.6 0.8 maximum_bitcast_fusion.h_ref
  39.3 47.7 %shard_map.59 = (f32[3,16,128]{2,1,0:T(8,128)}, f32[16,128]{1,0:T(8,128)}) custom-call(f32[3,64,256]{2,1,0:T(8,128)} %maximum_bitcast_fusion.h_ref, s32[40,128]{1,0:T(8,128)} %constant.6.clone.row_ref, s32[7,8,128]{2,1,0:T(8,128)} %constant.7.clone.tab_ref), custom_call_target="tpu_custom_call" | custom-call | tf_op jit(solution)/shard_map/pallas_call | solution.py:426
  (5 shorter events, 0.1 us)
Async XLA Ops:
  1.5 0.7 copy-start
  2.3 4.5 %collective-permute-start = (f32[3,4,4,64]{3,2,1,0:T(4,128)S(1)}, f32[3,4,4,64]{3,2,1,0:T(4,128)S(1)}, u32[]{:S(2)}, u32[]{:S(2)}) collective-permute-start(f32[3,4,4,64]{3,2,1,0:T(4,128)S(1)} %get-tuple-element.10), channel_id=1, source_target_pairs={{0,1},{1,2},{2,3},{3,4},{4,5},{5,6},{6,7},{7,0},{8,9},{9,10},{10,1... | collective-permute-start | bytes 36872 | tf_op jit(solution)/shard_map/ppermute | solution.py:454
  2.3 4.5 %collective-permute-start.1 = (f32[3,4,4,64]{3,2,1,0:T(4,128)S(1)}, f32[3,4,4,64]{3,2,1,0:T(4,128)S(1)}, u32[]{:S(2)}, u32[]{:S(2)}) collective-permute-start(f32[3,4,4,64]{3,2,1,0:T(4,128)S(1)} %get-tuple-element.11), channel_id=1, source_target_pairs={{1,0},{2,1},{3,2},{4,3},{5,4},{6,5},{7,6},{0,7},{9,8},{10,9},{11,1... | collective-permute-start | bytes 36872 | tf_op jit(solution)/shard_map/ppermute | solution.py:455
  6.9 20.6 %collective-permute-start.2 = (f32[3,2,4,256]{3,2,1,0:T(4,128)S(1)}, f32[3,2,4,256]{3,2,1,0:T(4,128)S(1)}, u32[]{:S(2)}, u32[]{:S(2)}) collective-permute-start(f32[3,2,4,256]{3,2,1,0:T(4,128)S(1)} %get-tuple-element.8), channel_id=1, source_target_pairs={{0,32},{32,64},{64,96},{96,128},{128,160},{160,192},{192,224},{224... | collective-permute-start | bytes 73736 | tf_op jit(solution)/shard_map/ppermute | solution.py:454
  10.8 18.3 %collective-permute-start.3 = (f32[3,2,4,256]{3,2,1,0:T(4,128)S(1)}, f32[3,2,4,256]{3,2,1,0:T(4,128)S(1)}, u32[]{:S(2)}, u32[]{:S(2)}) collective-permute-start(f32[3,2,4,256]{3,2,1,0:T(4,128)S(1)} %get-tuple-element.9), channel_id=1, source_target_pairs={{32,0},{64,32},{96,64},{128,96},{160,128},{192,160},{224,192},{256... | collective-permute-start | bytes 73736 | tf_op jit(solution)/shard_map/ppermute | solution.py:455
  29.2 6.0 %collective-permute-start.4 = (f32[3,8,2,256]{3,2,1,0:T(2,128)S(1)}, f32[3,8,2,256]{3,2,1,0:T(2,128)S(1)}, u32[]{:S(2)}, u32[]{:S(2)}) collective-permute-start(f32[3,8,2,256]{3,2,1,0:T(2,128)S(1)} %get-tuple-element.6), channel_id=1, source_target_pairs={{0,8},{8,16},{16,24},{24,0},{1,9},{9,17},{17,25},{25,1},{2,10},{10... | collective-permute-start | bytes 147464 | tf_op jit(solution)/shard_map/ppermute | solution.py:454
  31.4 7.2 %collective-permute-start.5 = (f32[3,8,2,256]{3,2,1,0:T(2,128)S(1)}, f32[3,8,2,256]{3,2,1,0:T(2,128)S(1)}, u32[]{:S(2)}, u32[]{:S(2)}) collective-permute-start(f32[3,8,2,256]{3,2,1,0:T(2,128)S(1)} %get-tuple-element.7), channel_id=1, source_target_pairs={{8,0},{16,8},{24,16},{0,24},{9,1},{17,9},{25,17},{1,25},{10,2},{18... | collective-permute-start | bytes 147464 | tf_op jit(solution)/shard_map/ppermute | solution.py:455

commit v3 on v2

--- a/solution.py
+++ b/solution.py
@@ -64,7 +64,8 @@
         ok = inside & (ce >= lo) & (ce < hi)
         back.append(np.where(ok, (ce - lo) * 8, 0) + sub)
         mask.append(np.broadcast_to(ok.astype(np.int32), (8, 128)))
-    fback = np.where(lane < 16, lane * 8, 0) + sub
+    own = (lane < 64) & (lane // 8 >= 2) & (lane // 8 < 6) & (lane % 8 >= 2) & (lane % 8 < 6)
+    fback = np.where(own, ((lane // 8 - 2) * 4 + lane % 8 - 2) * 8, 0) + sub
     return rows, np.stack(back + mask + [fback]).astype(np.int32)
 
 
@@ -155,7 +156,8 @@
 
 
 def kernel(h_ref, row_ref, tab_ref, force_ref, energy_ref,
-           dest_ref, tc_ref, tx_ref, rm_ref, rho_ref, sl_ref, em_ref, jd_ref, jf_ref, tf_ref):
+           dest_ref, tc_ref, tx_ref, rm_ref, rho_ref, sl_ref, em_ref, jd_ref, jf_ref, tf_ref,
+           nat_ref, oh_ref, lb_ref, oa_ref, os_ref):
     f32 = jnp.float32
     row = lax.broadcasted_iota(jnp.int32, (64, 256), 0)
     lane = lax.broadcasted_iota(jnp.int32, (64, 256), 1)
@@ -186,6 +188,10 @@
     orank = jnp.dot(jnp.where(over, 1.0, 0.0), upper, preferred_element_type=f32)
     novf = jnp.max(jnp.where(over, orank + 1.0, 0.0)).astype(jnp.int32)
     nch = (novf + 7) // 8
+    count = jnp.sum(jnp.where(over, 1.0, 0.0)).astype(jnp.int32)
+    slow = (nch > 1) | (count > 128)
+    nslow = jnp.where(slow, nch, 0)
+    quads = jnp.where(slow, 0, (count + 3) // 4)
     dest = jnp.where(over, orank + float(MAIN), bins * float(CAP) + rank)
     dest_ref[...] = jnp.where(valid, dest, -1.0)
 
@@ -289,8 +295,7 @@
         return acc
 
     def dens_rest(acc, it, t):
-        acc = dens_j(acc, it, t, NB, 1)
-        return lax.fori_loop(1, nch, lambda q, a: dens_j(a, it, t, NB + q, 1), acc)
+        return lax.fori_loop(0, nslow, lambda q, a: dens_j(a, it, t, NB + q, 1), acc)
 
     def dens_store(acc, t, ic, group=0):
         i8 = pl.multiple_of(ic * 8, 8)
@@ -322,10 +327,80 @@
         ic = NB + q
         it = dens_i(t, ic)
         acc = lax.fori_loop(0, 4, lambda g, a: dens_j(a, it, t, 7 * g, 7), zero)
-        acc = lax.fori_loop(0, nch, lambda p, a: dens_j(a, it, t, NB + p, 1), acc)
+        acc = lax.fori_loop(0, nslow, lambda p, a: dens_j(a, it, t, NB + p, 1), acc)
         dens_store(total(acc), t, ic)
 
-    pl.loop(0, 3 * nch)(dens_over)
+    pl.loop(0, 3 * nslow)(dens_over)
+
+    half = lane128 < 64
+    mlow = lax.broadcasted_iota(jnp.int32, (rows, 128), 1) < 64
+    for k in range(3):
+        front = tx_ref[k, 0:rows, 0:128]
+        full = front + pltpu.roll(front, 64, 1) + tx_ref[k, 0:rows, 128:256]
+        full = jnp.where(mlow, full, 0.0)
+        nat_ref[k, 0:rows, :] = full + pltpu.roll(full, 64, 1)
+    present = half & (tx_ref[0, MAIN : MAIN + 8, 0:128] < 0.5 * FAR)
+    lrow = lax.broadcasted_iota(jnp.int32, (128, 128), 0)
+
+    def over_rows(front, back):
+        return jnp.where(present, front + pltpu.roll(front, 64, 1) + back, 0.0)
+
+    def to_list(values, empty):
+        acc = jnp.zeros((128, 128), f32)
+        for r in range(8):
+            acc = acc + oh_ref[r] * values[r : r + 1, :]
+        acc = jnp.broadcast_to(jnp.sum(acc, axis=1, keepdims=True), (128, 128))
+        return jnp.where(lrow < count, acc, empty)
+
+    def list_pair(k, n, h):
+        i = 4 * n + 2 * h
+        one = jnp.broadcast_to(lb_ref[k, pl.ds(i, 1), :], (8, 128))
+        two = jnp.broadcast_to(lb_ref[k, pl.ds(i + 1, 1), :], (8, 128))
+        return jnp.where(half, one, two)
+
+    def keep_sums(k, value, n, h):
+        t = total(value)
+        i = 4 * n + 2 * h
+        os_ref[k, pl.ds(i, 1), :] = jnp.where(half, t, 0.0)[0:1]
+        os_ref[k, pl.ds(i + 1, 1), :] = jnp.where(half, 0.0, t)[0:1]
+
+    def from_list(k):
+        res = jnp.broadcast_to(jnp.sum(os_ref[k], axis=1, keepdims=True), (128, 128))
+        res = jnp.where(lrow < count, res, 0.0)
+        return jnp.concatenate([jnp.sum(oh_ref[r] * res, axis=0, keepdims=True) for r in range(8)], axis=0)
+
+    @pl.when(quads > 0)
+    def _():
+        there = jnp.where(present, 1.0, 0.0)
+        up = upper[0:128, 0:128]
+        before = jnp.dot(there, up, preferred_element_type=f32)
+        sums = jnp.dot(there, jnp.ones((128, 128), f32), preferred_element_type=f32)
+        tri = jnp.where(irow[0:8, 0:8] > ilane[0:8, 0:8], 1.0, 0.0)
+        place = jnp.where(present, before + jnp.dot(tri, sums, preferred_element_type=f32), -1.0)
+        lrowf = lrow.astype(f32)
+        for r in range(8):
+            oh_ref[r] = jnp.where(lrowf == place[r : r + 1, :], 1.0, 0.0)
+        for k in range(3):
+            lb_ref[k] = to_list(jnp.where(present, nat_ref[k, MAIN : MAIN + 8, :], 0.0), -FAR)
+        oa_ref[0] = jnp.zeros((rows, 128), f32)
+
+        def quad(n):
+            for h in range(2):
+                it = [list_pair(k, n, h) for k in range(3)]
+                own = zero
+                for m in range(NB + 1):
+                    vals = [nat_ref[k, 8 * m : 8 * m + 8, :] for k in range(3)]
+                    out = rho_tile(*it, *vals, m == NB)
+                    own = own + out
+                    if m < NB:
+                        oa_ref[0, 8 * m : 8 * m + 8, :] = oa_ref[0, 8 * m : 8 * m + 8, :] + out
+                keep_sums(0, own, n, h)
+
+        pl.loop(0, quads)(quad)
+        both = oa_ref[0, 0:MAIN, :]
+        rho_ref[0:MAIN, :] = rho_ref[0:MAIN, :] + both + pltpu.roll(both, 64, 1)
+        rho_ref[MAIN : MAIN + 8, :] = from_list(0)
+
 
     low = lax.broadcasted_iota(jnp.int32, (256, 128), 1) < 64
 
@@ -343,6 +418,9 @@
     def _():
         embed_rows(256)
 
+    sfront = sl_ref[0:rows, 0:128]
+    sfull = jnp.where(mlow, sfront + pltpu.roll(sfront, 64, 1) + sl_ref[0:rows, 128:256], 0.0)
+    nat_ref[3, 0:rows, :] = sfull + pltpu.roll(sfull, 64, 1)
     expand([sl_ref[0:rows, :]], W_FORC, 9, jf_ref, 4, (3,))
     expand_more([sl_ref], W_FORC, 9, jf_ref, 4, (3,), nch)
 
@@ -375,8 +453,7 @@
         ic = n + 6
         it = forc_i(ic)
         acc = forc_j(zeros5, it, n + 3, (0, 1, 3, 3, 3, 1, 0))
-        acc = forc_j(acc, it, NB, (3,))
-        acc = lax.fori_loop(1, nch, lambda q, a: forc_j(a, it, NB + q, (3,)), acc)
+        acc = lax.fori_loop(0, nslow, lambda q, a: forc_j(a, it, NB + q, (3,)), acc)
         forc_store(acc, it, ic)
 
     pl.loop(0, 16)(forc_main)
@@ -385,16 +462,51 @@
         ic = NB + q
         it = forc_i(ic)
         acc = lax.fori_loop(0, 5, lambda g, a: forc_j(a, it, 3 + 5 * g, (3,) * 5), zeros5)
-        acc = lax.fori_loop(0, nch, lambda p, a: forc_j(a, it, NB + p, (3,)), acc)
+        acc = lax.fori_loop(0, nslow, lambda p, a: forc_j(a, it, NB + p, (3,)), acc)
         forc_store(acc, it, ic)
 
-    pl.loop(0, nch)(forc_over)
+    pl.loop(0, nslow)(forc_over)
+
+    @pl.when(quads > 0)
+    def _():
+        lb_ref[3] = to_list(over_rows(sl_ref[MAIN : MAIN + 8, 0:128], sl_ref[MAIN : MAIN + 8, 128:256]), 0.0)
+        for k in range(4):
+            oa_ref[k] = jnp.zeros((rows, 128), f32)
+
+        def quad(n):
+            for h in range(2):
+                it = [list_pair(k, n, h) for k in range(4)]
+                own = [zero] * 4
+                for m in list(range(3, 25)) + [NB]:
+                    vals = [nat_ref[k, 8 * m : 8 * m + 8, :] for k in range(4)]
+                    fx, fy, fz, pv, rp = force_tile(*it, *vals, m == NB, 3)
+                    out = (fx, fy, fz, pv - TAPER_K * rp)
+                    own = [a + b for a, b in zip(own, out)]
+                    if m < NB:
+                        for k in range(4):
+                            old = oa_ref[k, 8 * m : 8 * m + 8, :]
+                            oa_ref[k, 8 * m : 8 * m + 8, :] = old - out[k] if k < 3 else old + out[k]
+                for k in range(4):
+                    keep_sums(k, own[k], n, h)
+
+        pl.loop(0, quads)(quad)
+        for k in range(4):
+            scale = SIGMA * 4.0 * TAPER_K if k < 3 else 0.5
+            both = oa_ref[k, 0:MAIN, :]
+            tf_ref[k, 0:MAIN, :] = tf_ref[k, 0:MAIN, :] + (both + pltpu.roll(both, 64, 1)) * scale
+            mine = from_list(k) * scale
+            if k == 3:
+                mine = mine + em_ref[MAIN : MAIN + 8, :]
+            tf_ref[k, MAIN : MAIN + 8, :] = jnp.where(present, mine, 0.0)
 
     row16 = lax.broadcasted_iota(jnp.int32, (16, 256), 0)
     oiota = lax.broadcasted_iota(jnp.int32, (256, 128), 0).astype(f32)
 
     def gather(half):
-        trans = [tf_ref[k, 256 * half : 256 * half + 256, :].T[0:16] for k in range(4)]
+        trans = []
+        for k in range(4):
+            flip = tf_ref[k, 256 * half : 256 * half + 256, :].T
+            trans.append(jnp.concatenate([flip[8 * x + 2 : 8 * x + 6] for x in range(2, 6)], axis=0))
         parts = [p for v in trans for p in split3(v)]
         acc = None
         for c in range(16):
@@ -439,6 +551,11 @@
             pltpu.VMEM((27, NCHUNK * 3, 8, 128), f32),
             pltpu.VMEM((9, NCHUNK * 4, 8, 128), f32),
             pltpu.VMEM((4, NSLOT, 128), f32),
+            pltpu.VMEM((4, MAIN + 8, 128), f32),
+            pltpu.VMEM((8, 128, 128), f32),
+            pltpu.VMEM((4, 128, 128), f32),
+            pltpu.VMEM((4, MAIN + 8, 128), f32),
+            pltpu.VMEM((4, 128, 128), f32),
         ],
         compiler_params=pltpu.CompilerParams(vmem_limit_bytes=60 * 1024 * 1024),
     )(halo, jnp.asarray(rows), jnp.asarray(tabs))

time: 87.5 us -> 85.1 us (0.973); the launches traced: 87 us -> 83.5 us
  Pallas kernels: 47.7 us -> 44.2 us
    pallas_call x1, Pallas kernels: 47.7 us -> 44.2 us  [local(): pl.pallas_call(kernel, out_shape=(jax.ShapeDtypeStruct((3, 16, 128), f32)...]
where the time goes in v3:
time: 85.1 us; the launch traced here: 83.5 us
  Pallas kernels  44.2 us (52%)
  starting transfers between devices  29.4 us (35%)
  waiting for transfers between devices  6.48 us (8%)
  local copies, waits for them, and re-layouts  1.72 us (2%)
  other arithmetic  1.01 us (1%)
    pallas_call x1, Pallas kernels, local(): pl.pallas_call(kernel, out_shape=(jax.ShapeDtypeStruct((3, 16, 128), f32)...  44.2 us
    ppermute x3, starting transfers between devices, with_halo(): after = lax.ppermute(first, axis, down)  23.4 us
    ppermute x3, starting transfers between devices, with_halo(): before = lax.ppermute(last, axis, up)  5.96 us
    ppermute x3, waiting for transfers between devices, with_halo(): after = lax.ppermute(first, axis, down)  4.85 us
  transfers between devices with their start and end apart: 6, of which 4 were waited for; matrix products, arithmetic and copies ran while one was open for 0% of the time, Pallas kernels for 0%

profile of v3, /device:TPU:24, one launch (start us, length us, event | category | flops | bytes accessed | tf_op | source)
XLA Modules:
  0.0 83.5 jit_solution(3468179024197919297)
XLA Ops:
  0.6 0.1 iota.12
  0.7 0.8 copy.6
  1.5 0.0 copy-start
  1.5 0.1 lt.14
  1.6 0.1 lt.15
  1.7 0.6 copy-done
  2.3 0.1 fusion.2
  2.3 0.0 collective-permute-start
  2.3 3.0 %collective-permute-start.1 = (f32[3,4,4,64]{3,2,1,0:T(4,128)S(1)}, f32[3,4,4,64]{3,2,1,0:T(4,128)S(1)}, u32[]{:S(2)}, u32[]{:S(2)}) collective-permute-start(f32[3,4,4,64]{3,2,1,0:T(4,128)S(1)} %get-tuple-element.11), channel_id=1, source_target_pairs={{1,0},{2,1},{3,2},{4,3},{5,4},{6,5},{7,6},{0,7},{9,8},{10,9},{11,1... | collective-permute-start | bytes 36872 | tf_op jit(solution)/shard_map/ppermute | solution.py:572
  5.3 1.5 %collective-permute-done = f32[3,4,4,64]{3,2,1,0:T(4,128)S(1)} collective-permute-done((f32[3,4,4,64]{3,2,1,0:T(4,128)S(1)}, f32[3,4,4,64]{3,2,1,0:T(4,128)S(1)}, u32[]{:S(2)}, u32[]{:S(2)}) %collective-permute-start) | collective-permute-done | bytes 12320 | tf_op jit(solution)/shard_map/ppermute | solution.py:571
  6.8 0.0 collective-permute-done.1
  6.8 0.1 pad_maximum_fusion.1
  6.9 3.8 %collective-permute-start.2 = (f32[3,2,4,256]{3,2,1,0:T(4,128)S(1)}, f32[3,2,4,256]{3,2,1,0:T(4,128)S(1)}, u32[]{:S(2)}, u32[]{:S(2)}) collective-permute-start(f32[3,2,4,256]{3,2,1,0:T(4,128)S(1)} %get-tuple-element.8), channel_id=1, source_target_pairs={{0,32},{32,64},{64,96},{96,128},{128,160},{160,192},{192,224},{224... | collective-permute-start | bytes 73736 | tf_op jit(solution)/shard_map/ppermute | solution.py:571
  10.8 16.8 %collective-permute-start.3 = (f32[3,2,4,256]{3,2,1,0:T(4,128)S(1)}, f32[3,2,4,256]{3,2,1,0:T(4,128)S(1)}, u32[]{:S(2)}, u32[]{:S(2)}) collective-permute-start(f32[3,2,4,256]{3,2,1,0:T(4,128)S(1)} %get-tuple-element.9), channel_id=1, source_target_pairs={{32,0},{64,32},{96,64},{128,96},{160,128},{192,160},{224,192},{256... | collective-permute-start | bytes 73736 | tf_op jit(solution)/shard_map/ppermute | solution.py:572
  27.6 0.0 collective-permute-done.2
  27.6 1.5 %collective-permute-done.3 = f32[3,2,4,256]{3,2,1,0:T(4,128)S(1)} collective-permute-done((f32[3,2,4,256]{3,2,1,0:T(4,128)S(1)}, f32[3,2,4,256]{3,2,1,0:T(4,128)S(1)}, u32[]{:S(2)}, u32[]{:S(2)}) %collective-permute-start.3) | collective-permute-done | bytes 24608 | tf_op jit(solution)/shard_map/ppermute | solution.py:572
  29.1 0.1 pad_maximum_fusion
  29.2 2.1 %collective-permute-start.4 = (f32[3,8,2,256]{3,2,1,0:T(2,128)S(1)}, f32[3,8,2,256]{3,2,1,0:T(2,128)S(1)}, u32[]{:S(2)}, u32[]{:S(2)}) collective-permute-start(f32[3,8,2,256]{3,2,1,0:T(2,128)S(1)} %get-tuple-element.6), channel_id=1, source_target_pairs={{0,8},{8,16},{16,24},{24,0},{1,9},{9,17},{17,25},{25,1},{2,10},{10... | collective-permute-start | bytes 147464 | tf_op jit(solution)/shard_map/ppermute | solution.py:571
  31.4 3.7 %collective-permute-start.5 = (f32[3,8,2,256]{3,2,1,0:T(2,128)S(1)}, f32[3,8,2,256]{3,2,1,0:T(2,128)S(1)}, u32[]{:S(2)}, u32[]{:S(2)}) collective-permute-start(f32[3,8,2,256]{3,2,1,0:T(2,128)S(1)} %get-tuple-element.7), channel_id=1, source_target_pairs={{8,0},{16,8},{24,16},{0,24},{9,1},{17,9},{25,17},{1,25},{10,2},{18... | collective-permute-start | bytes 147464 | tf_op jit(solution)/shard_map/ppermute | solution.py:572
  35.1 0.1 collective-permute-done.4
  35.2 3.3 %collective-permute-done.5 = f32[3,8,2,256]{3,2,1,0:T(2,128)S(1)} collective-permute-done((f32[3,8,2,256]{3,2,1,0:T(2,128)S(1)}, f32[3,8,2,256]{3,2,1,0:T(2,128)S(1)}, u32[]{:S(2)}, u32[]{:S(2)}) %collective-permute-start.5) | collective-permute-done | bytes 49184 | tf_op jit(solution)/shard_map/ppermute | solution.py:572
  38.6 0.8 maximum_bitcast_fusion.h_ref
  39.3 44.2 %shard_map.59 = (f32[3,16,128]{2,1,0:T(8,128)}, f32[16,128]{1,0:T(8,128)}) custom-call(f32[3,64,256]{2,1,0:T(8,128)} %maximum_bitcast_fusion.h_ref, s32[40,128]{1,0:T(8,128)} %constant.6.clone.row_ref, s32[7,8,128]{2,1,0:T(8,128)} %constant.7.clone.tab_ref), custom_call_target="tpu_custom_call" | custom-call | tf_op jit(solution)/shard_map/pallas_call | solution.py:538
  (5 shorter events, 0.1 us)
Async XLA Ops:
  1.5 0.7 copy-start
  2.3 4.5 %collective-permute-start = (f32[3,4,4,64]{3,2,1,0:T(4,128)S(1)}, f32[3,4,4,64]{3,2,1,0:T(4,128)S(1)}, u32[]{:S(2)}, u32[]{:S(2)}) collective-permute-start(f32[3,4,4,64]{3,2,1,0:T(4,128)S(1)} %get-tuple-element.10), channel_id=1, source_target_pairs={{0,1},{1,2},{2,3},{3,4},{4,5},{5,6},{6,7},{7,0},{8,9},{9,10},{10,1... | collective-permute-start | bytes 36872 | tf_op jit(solution)/shard_map/ppermute | solution.py:571
  2.3 4.5 %collective-permute-start.1 = (f32[3,4,4,64]{3,2,1,0:T(4,128)S(1)}, f32[3,4,4,64]{3,2,1,0:T(4,128)S(1)}, u32[]{:S(2)}, u32[]{:S(2)}) collective-permute-start(f32[3,4,4,64]{3,2,1,0:T(4,128)S(1)} %get-tuple-element.11), channel_id=1, source_target_pairs={{1,0},{2,1},{3,2},{4,3},{5,4},{6,5},{7,6},{0,7},{9,8},{10,9},{11,1... | collective-permute-start | bytes 36872 | tf_op jit(solution)/shard_map/ppermute | solution.py:572
  6.9 20.6 %collective-permute-start.2 = (f32[3,2,4,256]{3,2,1,0:T(4,128)S(1)}, f32[3,2,4,256]{3,2,1,0:T(4,128)S(1)}, u32[]{:S(2)}, u32[]{:S(2)}) collective-permute-start(f32[3,2,4,256]{3,2,1,0:T(4,128)S(1)} %get-tuple-element.8), channel_id=1, source_target_pairs={{0,32},{32,64},{64,96},{96,128},{128,160},{160,192},{192,224},{224... | collective-permute-start | bytes 73736 | tf_op jit(solution)/shard_map/ppermute | solution.py:571
  10.8 18.3 %collective-permute-start.3 = (f32[3,2,4,256]{3,2,1,0:T(4,128)S(1)}, f32[3,2,4,256]{3,2,1,0:T(4,128)S(1)}, u32[]{:S(2)}, u32[]{:S(2)}) collective-permute-start(f32[3,2,4,256]{3,2,1,0:T(4,128)S(1)} %get-tuple-element.9), channel_id=1, source_target_pairs={{32,0},{64,32},{96,64},{128,96},{160,128},{192,160},{224,192},{256... | collective-permute-start | bytes 73736 | tf_op jit(solution)/shard_map/ppermute | solution.py:572
  29.2 6.0 %collective-permute-start.4 = (f32[3,8,2,256]{3,2,1,0:T(2,128)S(1)}, f32[3,8,2,256]{3,2,1,0:T(2,128)S(1)}, u32[]{:S(2)}, u32[]{:S(2)}) collective-permute-start(f32[3,8,2,256]{3,2,1,0:T(2,128)S(1)} %get-tuple-element.6), channel_id=1, source_target_pairs={{0,8},{8,16},{16,24},{24,0},{1,9},{9,17},{17,25},{25,1},{2,10},{10... | collective-permute-start | bytes 147464 | tf_op jit(solution)/shard_map/ppermute | solution.py:571
  31.4 7.2 %collective-permute-start.5 = (f32[3,8,2,256]{3,2,1,0:T(2,128)S(1)}, f32[3,8,2,256]{3,2,1,0:T(2,128)S(1)}, u32[]{:S(2)}, u32[]{:S(2)}) collective-permute-start(f32[3,8,2,256]{3,2,1,0:T(2,128)S(1)} %get-tuple-element.7), channel_id=1, source_target_pairs={{8,0},{16,8},{24,16},{0,24},{9,1},{17,9},{25,17},{1,25},{10,2},{18... | collective-permute-start | bytes 147464 | tf_op jit(solution)/shard_map/ppermute | solution.py:572

commit v4 on v3

--- a/solution.py
+++ b/solution.py
@@ -303,12 +303,19 @@
         rho_ref[pl.ds(i8, 8), :] = jnp.where(tab_ref[T_MASK + t] > 0, got, rho_ref[pl.ds(i8, 8), :])
 
     def dens_main(n):
-        e, t = n // 2, n % 2
-        it = dens_i(t, e + 3)
-        acc = dens_rest(dens_j(zero, it, t, e, 7), it, t)
-        dens_store(total(acc), t, e + 3)
-
-    pl.loop(0, 44)(dens_main)
+        e, t = 2 * (n // 2), n % 2
+        its = [dens_i(t, e + 3 + v) for v in range(2)]
+        accs = [zero, zero]
+        for m in range(8):
+            for s in range(9):
+                vals = [jd_ref[9 * t + s, (e + m) * 3 + k] for k in range(3)]
+                for v in range(2):
+                    if 0 <= m - v < 7:
+                        accs[v] = accs[v] + rho_tile(*its[v], *vals, s == 4)
+        for v in range(2):
+            dens_store(total(dens_rest(accs[v], its[v], t)), t, e + 3 + v)
+
+    pl.loop(0, 22)(dens_main)
 
     def dens_corner(n):
         e = jnp.minimum(4 * n, 18)
@@ -579,7 +586,14 @@
     slot = lax.broadcasted_iota(jnp.int32, (cx, cy, cz, SLOTS), 3)
     occupied = (slot < counts[..., None]).reshape(1, cx, cy, cz * SLOTS)
     packed = jnp.where(occupied, positions, 1.0e6)
-    halo = with_halo(packed, (("gz", 3, SLOTS), ("gx", 1, 2), ("gy", 2, 2)))
+    halo = with_halo(packed, (("gz", 3, SLOTS), ("gx", 1, 2)))
+    here, count = lax.axis_index("gy"), lax.axis_size("gy")
+    peer = lax.broadcasted_iota(jnp.int32, (count, 1, 1, 1, 1), 0)
+    send = jnp.where((peer - here + count) % count == 1, halo[None, :, :, cy - 2 :], halo[None, :, :, :2])
+    got = lax.all_to_all(send, "gy", 0, 0)
+    before = lax.dynamic_index_in_dim(got, (here + count - 1) % count, 0, keepdims=False)
+    after = lax.dynamic_index_in_dim(got, (here + 1) % count, 0, keepdims=False)
+    halo = jnp.concatenate([before, halo, after], axis=2)
     forces, energy = local(halo.reshape(3, 64, 256))
     return forces.reshape(3, cx, cy, cz * SLOTS), energy.reshape(cx, cy, cz * SLOTS)
 

time: 85.1 us -> 87.6 us (1.029)
  the two profiles are of different devices: /device:TPU:24 before, /device:TPU:3 now
where the time goes in v4:
time: 87.6 us; the launch traced here: 87.1 us
  Pallas kernels  46.3 us (53%)
  starting transfers between devices  26.3 us (30%)
  waiting for transfers between devices  10.2 us (12%)
  other arithmetic  1.85 us (2%)
  local copies, waits for them, and re-layouts  1.73 us (2%)
    pallas_call x1, Pallas kernels, local(): pl.pallas_call(kernel, out_shape=(jax.ShapeDtypeStruct((3, 16, 128), f32)...  46.3 us
    ppermute x2, starting transfers between devices, with_halo(): after = lax.ppermute(first, axis, down)  16.8 us
    all_to_all x1, waiting for transfers between devices, on_device(): got = lax.all_to_all(send, 'gy', 0, 0)  6.01 us
    ppermute x2, starting transfers between devices, with_halo(): before = lax.ppermute(last, axis, up)  5.32 us
    all_to_all x1, starting transfers between devices, on_device(): got = lax.all_to_all(send, 'gy', 0, 0)  4.18 us
    ppermute x2, waiting for transfers between devices, with_halo(): after = lax.ppermute(first, axis, down)  3.2 us
  transfers between devices with their start and end apart: 5, of which 4 were waited for; matrix products, arithmetic and copies ran while one was open for 0% of the time, Pallas kernels for 0%

profile of v4, /device:TPU:3, one launch (start us, length us, event | category | flops | bytes accessed | tf_op | source)
XLA Modules:
  0.0 87.1 jit_solution(13244063152586260239)
XLA Ops:
  0.6 0.8 copy.6
  1.4 0.1 lt.38
  1.5 0.0 copy-start
  1.5 0.1 lt.39
  1.6 0.1 iota.19
  1.7 0.6 copy-done
  2.3 0.1 fusion.4
  2.3 1.8 %collective-permute-start = (f32[3,4,4,64]{3,2,1,0:T(4,128)S(1)}, f32[3,4,4,64]{3,2,1,0:T(4,128)S(1)}, u32[]{:S(2)}, u32[]{:S(2)}) collective-permute-start(f32[3,4,4,64]{3,2,1,0:T(4,128)S(1)} %get-tuple-element.12), channel_id=1, source_target_pairs={{0,1},{1,2},{2,3},{3,4},{4,5},{5,6},{6,7},{7,0},{8,9},{9,10},{10,1... | collective-permute-start | bytes 36872 | tf_op jit(solution)/shard_map/ppermute | solution.py:578
  4.1 0.0 collective-permute-start.1
  4.1 0.9 %collective-permute-done = f32[3,4,4,64]{3,2,1,0:T(4,128)S(1)} collective-permute-done((f32[3,4,4,64]{3,2,1,0:T(4,128)S(1)}, f32[3,4,4,64]{3,2,1,0:T(4,128)S(1)}, u32[]{:S(2)}, u32[]{:S(2)}) %collective-permute-start) | collective-permute-done | bytes 12320 | tf_op jit(solution)/shard_map/ppermute | solution.py:578
  5.1 2.3 %collective-permute-done.1 = f32[3,4,4,64]{3,2,1,0:T(4,128)S(1)} collective-permute-done((f32[3,4,4,64]{3,2,1,0:T(4,128)S(1)}, f32[3,4,4,64]{3,2,1,0:T(4,128)S(1)}, u32[]{:S(2)}, u32[]{:S(2)}) %collective-permute-start.1) | collective-permute-done | bytes 12320 | tf_op jit(solution)/shard_map/ppermute | solution.py:579
  7.4 0.1 pad_maximum_fusion.1
  7.5 3.5 %collective-permute-start.2 = (f32[3,2,4,256]{3,2,1,0:T(4,128)S(1)}, f32[3,2,4,256]{3,2,1,0:T(4,128)S(1)}, u32[]{:S(2)}, u32[]{:S(2)}) collective-permute-start(f32[3,2,4,256]{3,2,1,0:T(4,128)S(1)} %get-tuple-element.10), channel_id=1, source_target_pairs={{0,32},{32,64},{64,96},{96,128},{128,160},{160,192},{192,224},{224... | collective-permute-start | bytes 73736 | tf_op jit(solution)/shard_map/ppermute | solution.py:578
  11.0 16.8 %collective-permute-start.3 = (f32[3,2,4,256]{3,2,1,0:T(4,128)S(1)}, f32[3,2,4,256]{3,2,1,0:T(4,128)S(1)}, u32[]{:S(2)}, u32[]{:S(2)}) collective-permute-start(f32[3,2,4,256]{3,2,1,0:T(4,128)S(1)} %get-tuple-element.11), channel_id=1, source_target_pairs={{32,0},{64,32},{96,64},{128,96},{160,128},{192,160},{224,192},{256... | collective-permute-start | bytes 73736 | tf_op jit(solution)/shard_map/ppermute | solution.py:579
  27.8 0.0 collective-permute-done.2
  27.9 0.9 %collective-permute-done.3 = f32[3,2,4,256]{3,2,1,0:T(4,128)S(1)} collective-permute-done((f32[3,2,4,256]{3,2,1,0:T(4,128)S(1)}, f32[3,2,4,256]{3,2,1,0:T(4,128)S(1)}, u32[]{:S(2)}, u32[]{:S(2)}) %collective-permute-start.3) | collective-permute-done | bytes 24608 | tf_op jit(solution)/shard_map/ppermute | solution.py:579
  28.8 0.1 pad_maximum_fusion
  28.9 0.8 broadcast_select_fusion
  29.7 4.2 %all-to-all-start = ((f32[4,3,8,2,256]{4,3,2,1,0:T(2,128)}), f32[4,3,8,2,256]{4,3,2,1,0:T(2,128)S(1)}, u32[]{:S(2)}, u32[]{:S(2)}) async-start(f32[4,3,8,2,256]{4,3,2,1,0:T(2,128)} %broadcast_select_fusion), calls=%async_computation | async-start | bytes 393216 | tf_op jit(solution)/shard_map/all_to_all | solution.py:593
  33.9 6.0 %all-to-all-done = f32[4,3,8,2,256]{4,3,2,1,0:T(2,128)S(1)} async-done(((f32[4,3,8,2,256]{4,3,2,1,0:T(2,128)}), f32[4,3,8,2,256]{4,3,2,1,0:T(2,128)S(1)}, u32[]{:S(2)}, u32[]{:S(2)}) %all-to-all-start) | async-done | bytes 196640 | tf_op jit(solution)/shard_map/all_to_all | solution.py:593
  39.9 0.8 maximum_bitcast_fusion.h_ref
  40.7 46.3 %shard_map.59 = (f32[3,16,128]{2,1,0:T(8,128)}, f32[16,128]{1,0:T(8,128)}) custom-call(f32[3,64,256]{2,1,0:T(8,128)} %maximum_bitcast_fusion.h_ref, s32[40,128]{1,0:T(8,128)} %constant.48.clone.row_ref, s32[7,8,128]{2,1,0:T(8,128)} %constant.49.clone.tab_ref), custom_call_target="tpu_custom_call" | custom-call | tf_op jit(solution)/shard_map/pallas_call | solution.py:545
  (7 shorter events, 0.1 us)
Async XLA Ops:
  1.5 0.7 copy-start
  2.3 2.7 %collective-permute-start = (f32[3,4,4,64]{3,2,1,0:T(4,128)S(1)}, f32[3,4,4,64]{3,2,1,0:T(4,128)S(1)}, u32[]{:S(2)}, u32[]{:S(2)}) collective-permute-start(f32[3,4,4,64]{3,2,1,0:T(4,128)S(1)} %get-tuple-element.12), channel_id=1, source_target_pairs={{0,1},{1,2},{2,3},{3,4},{4,5},{5,6},{6,7},{7,0},{8,9},{9,10},{10,1... | collective-permute-start | bytes 36872 | tf_op jit(solution)/shard_map/ppermute | solution.py:578
  4.1 3.3 %collective-permute-start.1 = (f32[3,4,4,64]{3,2,1,0:T(4,128)S(1)}, f32[3,4,4,64]{3,2,1,0:T(4,128)S(1)}, u32[]{:S(2)}, u32[]{:S(2)}) collective-permute-start(f32[3,4,4,64]{3,2,1,0:T(4,128)S(1)} %get-tuple-element.13), channel_id=1, source_target_pairs={{1,0},{2,1},{3,2},{4,3},{5,4},{6,5},{7,6},{0,7},{9,8},{10,9},{11,1... | collective-permute-start | bytes 36872 | tf_op jit(solution)/shard_map/ppermute | solution.py:579
  7.5 20.4 %collective-permute-start.2 = (f32[3,2,4,256]{3,2,1,0:T(4,128)S(1)}, f32[3,2,4,256]{3,2,1,0:T(4,128)S(1)}, u32[]{:S(2)}, u32[]{:S(2)}) collective-permute-start(f32[3,2,4,256]{3,2,1,0:T(4,128)S(1)} %get-tuple-element.10), channel_id=1, source_target_pairs={{0,32},{32,64},{64,96},{96,128},{128,160},{160,192},{192,224},{224... | collective-permute-start | bytes 73736 | tf_op jit(solution)/shard_map/ppermute | solution.py:578
  11.0 17.7 %collective-permute-start.3 = (f32[3,2,4,256]{3,2,1,0:T(4,128)S(1)}, f32[3,2,4,256]{3,2,1,0:T(4,128)S(1)}, u32[]{:S(2)}, u32[]{:S(2)}) collective-permute-start(f32[3,2,4,256]{3,2,1,0:T(4,128)S(1)} %get-tuple-element.11), channel_id=1, source_target_pairs={{32,0},{64,32},{96,64},{128,96},{160,128},{192,160},{224,192},{256... | collective-permute-start | bytes 73736 | tf_op jit(solution)/shard_map/ppermute | solution.py:579
  29.7 10.2 %all-to-all-start = ((f32[4,3,8,2,256]{4,3,2,1,0:T(2,128)}), f32[4,3,8,2,256]{4,3,2,1,0:T(2,128)S(1)}, u32[]{:S(2)}, u32[]{:S(2)}) async-start(f32[4,3,8,2,256]{4,3,2,1,0:T(2,128)} %broadcast_select_fusion), calls=%async_computation | async-start | bytes 393216 | tf_op jit(solution)/shard_map/all_to_all | solution.py:593
